TPU v7x, 256 devices: a whole 4x4x8 slice. The times are simulated.
256 devices in a mesh: base: 32 (over x, z_lo, core), chan: 8 (over y, z_hi).
Axes of the slice: x: 4, y: 4, z: 8 (z_hi: 2, z_lo: 4; z = z_hi * 4 + z_lo), core: 2. Of those that a mesh axis runs over, the one named last changes fastest.
Arguments:
- image0: float32 [2048, 2048], P(('base', 'chan')), may hold values from -6 to 6
- interp: float32 [32, 8, 256, 8, 256], P('base', 'chan'), may hold values from -0.375 to 0.375
- vis_weight: float32 [32, 8, 256, 8], P('base', 'chan'), may hold values from 0.2 to 5
- counts: int32 [32, 8, 256], P('base', 'chan'), may hold values from 1 to 8
- tile_index: int32 [32, 8, 256], P('base', 'chan'), may hold values from 0 to 63
Outputs:
- image_out: float32 [2048, 2048], P(('base', 'chan'))
- estimates: float32 [3], replicated
Inputs may be any that keep to these rules, and one draw needn't show every extreme that they name: `tile_index`: slot s of a device belongs to the spectrum block of device s // 1 of base+chan, base index major; the entry numbers the tile within that block. `counts`: visibility v of a slot is live when v < count.
All inputs are finite; a program needn't handle non-finite values.
Results may differ from a plain program's by a relative error of at most 0.00023.
Values sent between devices are 32-bit elements; how exact they have to be, the bound alone decides.
No kernel may reach another device: no remote copies, remote signals or barrier semaphores. Data moves between devices by JAX's collectives and lax.ppermute only.
A program may use at most 64 MiB of HBM per device.

v0:
```python
import functools
import math

import jax
import jax.numpy as jnp
import ml_dtypes
import numpy as np
from jax import lax
from jax.experimental import pallas as pl
from jax.experimental.pallas import tpu as pltpu
from jax.sharding import PartitionSpec as P

AXES = ("base", "chan")
N = 2048
DEV = 256
ROWS = 8
CELLS = 256
SLOTS = 256
VCAP = 8
SAMPLES = SLOTS * VCAP
LANES = 128
MSG = 18
GROUP = 4
START_SCALE = 2.0**-11
NORM_LANE = 40
F32 = jnp.float32
BF16 = jnp.bfloat16
VMEM = pl.BlockSpec(memory_space=pltpu.VMEM)
ANY = pl.BlockSpec(memory_space=pl.ANY)


def chip_path():
    path = []
    for x in range(4):
        for step_y, y in enumerate(range(4) if x % 2 == 0 else range(3, -1, -1)):
            zs = range(8) if (x * 4 + step_y) % 2 == 0 else range(7, -1, -1)
            path.extend((x, y, z) for z in zs)
    return path


def block_places():
    places = [0] * DEV
    for o, (x, y, z) in enumerate(chip_path()):
        for core in range(2):
            place = (x * 8 + z % 4 * 2 + core) * 8 + y * 2 + z // 4
            places[o if core == 0 else DEV - 1 - o] = place
    return places


PLACES = block_places()
MIRROR = [(PLACES[o], PLACES[DEV - 1 - o]) for o in range(DEV)]
MIRROR_EDGE = [(PLACES[o], PLACES[(DEV - o) % DEV]) for o in range(DEV)]


def halves(table):
    high = table.astype(ml_dtypes.bfloat16)
    low = (table - high.astype(np.float64)).astype(ml_dtypes.bfloat16)
    return high, low


def turns(products, modulus):
    angle = 2.0 * np.pi * (np.asarray(products) % modulus) / modulus
    return np.cos(angle), np.sin(angle)


@functools.cache
def tables():
    out = {}
    index = np.arange(DEV)
    for name, rows in (("plain", index), ("placed", np.array(PLACES))):
        cos, sin = turns(rows[:, None] * index[None, :], DEV)
        out[name] = halves(np.concatenate([cos, sin], axis=1))
    small = np.arange(8)
    cos, sin = turns(small[:, None] * index[None, :], N)
    out["turn"] = np.concatenate([cos, sin], axis=0).astype(np.float32)
    cos8, sin8 = turns(small[:, None] * small[None, :], 8)
    eye = np.eye(8)
    cos, sin = np.kron(eye, cos8), np.kron(eye, sin8)
    out["eight_fwd"] = halves(np.block([[cos, sin], [-sin, cos]]))
    out["eight_inv"] = halves(np.block([[cos, -sin], [sin, cos]]))
    row = np.arange(64)
    tile = row % 8 * 8 + row // 8
    place = np.argsort(tile)
    flips = []
    for source in (63 - tile, (64 - tile) % 64):
        one = np.zeros((64, 64))
        one[row, place[source]] = 1.0
        flips.append(np.kron(np.diag([1.0, -1.0]), one))
    out["flip_tile"] = np.concatenate(flips, axis=0).astype(ml_dtypes.bfloat16)
    cell = np.arange(CELLS)
    target = (8 - cell // 32) % 8 * 32 + (32 - cell % 32) % 32
    flip = np.zeros((CELLS, CELLS))
    flip[target, cell] = 1.0
    out["flip_cell"] = flip.astype(ml_dtypes.bfloat16)
    spread = (index[:, None] % 32 == index[None, :] // 8).astype(ml_dtypes.bfloat16)
    out["spread"] = spread
    share = np.zeros((DEV, 8))
    share[: DEV // 2, :4] = 2.0
    share[DEV // 2 :, 1:5] = 2.0
    share[0, 0] = 1.0
    share[DEV // 2, 0] = 1.0
    share = np.repeat(share, ROWS, axis=1)
    out["share"] = np.concatenate([share, share], axis=1).astype(np.float32)
    return out


def split(x):
    high = x.astype(BF16)
    return high, (x - high.astype(F32)).astype(BF16)


def dot(a, b, dims=((1,), (0,))):
    return lax.dot_general(a, b, (dims, ((), ())), preferred_element_type=F32)


def dot3(a, b, dims=((1,), (0,))):
    (ah, al), (bh, bl) = a, b
    return dot(ah, bh, dims) + (dot(ah, bl, dims) + dot(al, bh, dims))


NT = ((1,), (1,))


def load_pair(high_ref, low_ref):
    return high_ref[...], low_ref[...]


def swap_chunks(x):
    chunk = lax.broadcasted_iota(jnp.int32, (8, LANES), 1) // 32
    blocks = {}
    for part in range(2):
        for a_high in range(2):
            for b_high in range(2):
                source = [
                    x[
                        part * 64 + (a_high * 4 + a) * 8 : part * 64 + (a_high * 4 + a) * 8 + 8,
                        b_high * LANES : (b_high + 1) * LANES,
                    ]
                    for a in range(4)
                ]
                for b in range(4):
                    made = None
                    for a in range(4):
                        shift = (a - b) * 32 % LANES
                        moved = source[a] if shift == 0 else pltpu.roll(source[a], shift, 1)
                        made = moved if made is None else jnp.where(chunk == a, moved, made)
                    blocks[part, b_high * 4 + b, a_high] = made
    rows = [
        jnp.concatenate([blocks[part, b, 0], blocks[part, b, 1]], axis=1)
        for part in range(2)
        for b in range(8)
    ]
    return jnp.concatenate(rows, axis=0)


def fold(x):
    squares = x * x
    total = None
    for i in range(x.shape[0] // 8):
        for j in range(x.shape[1] // LANES):
            piece = squares[i * 8 : i * 8 + 8, j * LANES : (j + 1) * LANES]
            total = piece if total is None else total + piece
    return total


def apply_matrix(spectrum, ah_ref, al_ref, mask_ref):
    parts = split(spectrum)
    row = lax.broadcasted_iota(jnp.int32, (LANES, 256), 0)
    tile = (row % 8 * 8 + row // 8 % 8).astype(F32)
    total = None
    for m in range(SAMPLES // 256):
        a = (ah_ref[pl.ds(m * 256, 256), :], al_ref[pl.ds(m * 256, 256), :])
        seen = dot3(parts, a, NT)
        weight = mask_ref[m : m + 1, :]
        wanted = mask_ref[8 + m : 9 + m, :]
        kept = jnp.where(tile == wanted, seen * weight, 0.0)
        added = dot3(split(kept), a)
        total = added if total is None else total + added
    return total


def mirrored(own_ref, other_ref, edge_ref, flip_tile_ref, flip_cell_ref):
    lane = lax.broadcasted_iota(jnp.int32, (LANES, CELLS), 1)
    other = other_ref[...]
    edge = jnp.concatenate([edge_ref[...], other[:, LANES:]], axis=1)
    other = jnp.where(lane < 32, edge, other)
    high, low = split(other)
    flips = flip_tile_ref[...]
    turned = dot(flips, high) + dot(flips, low)
    turned = jnp.where(lane % 32 == 0, turned[LANES:], turned[:LANES])
    high, low = split(turned)
    flip = flip_cell_ref[...]
    return 0.5 * (own_ref[...] + (dot(high, flip) + dot(low, flip)))


def pack_kernel(image_ref, interp_ref, weight_ref, marks_ref, th_ref, tl_ref, turn_ref,
                out_ref, norm_ref, held, extra, sems):
    pieces = 4
    size = SLOTS // pieces
    copies = [
        pltpu.make_async_copy(
            interp_ref.at[pl.ds(i * size, size)], held.at[pl.ds(i * size, size)], sems.at[i]
        )
        for i in range(pieces)
    ]
    for copy in copies:
        copy.start()
    image = image_ref[...]
    x = [image[:, q * 256 : (q + 1) * 256] for q in range(8)]
    squares = None
    for q in range(8):
        both = x[q][:, :LANES] ** 2 + x[q][:, LANES:] ** 2
        squares = both if squares is None else squares + both
    norm_ref[...] = squares
    re, im = [None] * 8, [None] * 8
    for c in range(5):
        cos = [math.cos(2.0 * math.pi * (c * q % 8) / 8) for q in range(8)]
        sin = [math.sin(2.0 * math.pi * (c * q % 8) / 8) for q in range(8)]
        re[c] = sum(x[q] * cos[q] for q in range(1, 8)) + x[0]
        im[c] = jnp.zeros_like(x[0]) if c % 4 == 0 else -sum(x[q] * sin[q] for q in range(1, 8))
        if 0 < c < 4:
            re[8 - c] = re[c]
            im[8 - c] = -im[c]
    turned_re, turned_im = [], []
    for c in range(8):
        cos, sin = turn_ref[c : c + 1, :], turn_ref[8 + c : 9 + c, :]
        turned_re.append(re[c] * cos + im[c] * sin)
        turned_im.append(im[c] * cos - re[c] * sin)
    plain = jnp.concatenate(turned_re + turned_im, axis=0)
    crossed = jnp.concatenate(turned_im + [-v for v in turned_re], axis=0)
    data = split(jnp.concatenate([plain, crossed], axis=1))
    columns = dot3(load_pair(th_ref, tl_ref), data, NT)
    out_ref[pl.ds(16, DEV, stride=MSG), :] = columns
    marks = jnp.concatenate(
        [jnp.zeros((8, SLOTS), F32), marks_ref[...], jnp.zeros((LANES - 16, SLOTS), F32)], axis=0
    )
    extra[...] = marks.T
    extra[:, :VCAP] = weight_ref[...]
    out_ref[pl.ds(17, DEV, stride=MSG), :] = extra[...]

    def move(group, carry):
        base = pl.multiple_of(group * (GROUP * MSG), 8)
        for m in range(GROUP):
            for tile in range(2):
                out_ref[pl.ds(base + m * MSG + tile * 8, 8), :] = held[
                    group * GROUP + m, :, tile * LANES : (tile + 1) * LANES
                ]
        return carry

    groups = SLOTS // GROUP // pieces
    for i in range(pieces):
        copies[i].wait()
        lax.fori_loop(i * groups, (i + 1) * groups, move, 0, unroll=2)


def first_kernel(got_ref, th_ref, tl_ref, turn_ref, eh_ref, el_ref, spread_ref,
                 out_ref, ah_ref, al_ref, mask_ref):
    def unpack(group, carry):
        base = pl.multiple_of(group * (GROUP * MSG), 8)
        for pair in range(GROUP // 2):
            rows = []
            for m in (2 * pair, 2 * pair + 1):
                rows.append(
                    jnp.concatenate(
                        [got_ref[pl.ds(base + m * MSG + t * 8, 8), :] for t in range(2)], axis=1
                    )
                )
            high, low = split(jnp.concatenate(rows, axis=0))
            start = pl.multiple_of(group * 32 + pair * 16, 16)
            ah_ref[pl.ds(start, 16), :] = high
            al_ref[pl.ds(start, 16), :] = low
        return carry

    lax.fori_loop(0, SLOTS // GROUP, unpack, 0, unroll=2)

    marks = got_ref[pl.ds(17, DEV, stride=MSG), :].T[:16]
    chunk = lax.broadcasted_iota(jnp.int32, (16, SLOTS), 1) // 32
    stacked = jnp.concatenate([jnp.where(chunk == m, marks, 0.0) for m in range(8)], axis=0)
    high, low = split(stacked)
    lowest = (stacked - high.astype(F32) - low.astype(F32)).astype(BF16)
    spread = spread_ref[...]
    spread_marks = dot(high, spread) + (dot(low, spread) + dot(lowest, spread))
    sample = lax.broadcasted_iota(jnp.int32, (8, 256), 1) % 8
    row = lax.broadcasted_iota(jnp.int32, (8, 256), 0)
    for m in range(8):
        block = spread_marks[m * 16 : m * 16 + 16]
        weight = jnp.sum(jnp.where(sample == row, block[:8], 0.0), axis=0, keepdims=True)
        live = sample[:1].astype(F32) < block[9:10]
        mask_ref[m : m + 1, :] = jnp.where(live, weight, 0.0)
        mask_ref[8 + m : 9 + m, :] = block[8:9]

    columns = got_ref[pl.ds(16, DEV, stride=MSG), :].T
    both = dot3(split(columns), load_pair(th_ref, tl_ref))
    by_cos, by_sin = both[:, :DEV], both[:, DEV:]
    re = (by_cos[:64] + by_sin[64:]).reshape(8, 8, DEV)
    im = (by_cos[64:] - by_sin[:64]).reshape(8, 8, DEV)
    scale = START_SCALE / N
    cos, sin = turn_ref[:8, :] * scale, turn_ref[8:, :] * scale
    turned = jnp.concatenate([re * cos + im * sin, im * cos - re * sin], axis=0)
    spectrum = dot3(load_pair(eh_ref, el_ref), split(turned.reshape(LANES, DEV)))
    out_ref[...] = apply_matrix(swap_chunks(spectrum), ah_ref, al_ref, mask_ref)


def next_kernel(own_ref, other_ref, edge_ref, ah_ref, al_ref, mask_ref, ft_ref, fc_ref,
                out_ref, norm_ref):
    spectrum = mirrored(own_ref, other_ref, edge_ref, ft_ref, fc_ref)
    norm_ref[...] = fold(spectrum)
    out_ref[...] = apply_matrix(spectrum, ah_ref, al_ref, mask_ref)


def send_kernel(own_ref, other_ref, edge_ref, n0_ref, n1_ref, n2_ref, ft_ref, fc_ref,
                th_ref, tl_ref, turn_ref, eh_ref, el_ref, out_ref):
    spectrum = mirrored(own_ref, other_ref, edge_ref, ft_ref, fc_ref)
    norms = [jnp.sum(n) for n in (n0_ref[...], n1_ref[...], n2_ref[...], fold(spectrum))]
    data = dot3(load_pair(eh_ref, el_ref), split(swap_chunks(spectrum)))
    re = data[:64].reshape(8, 8, DEV)
    im = data[64:].reshape(8, 8, DEV)
    cos, sin = turn_ref[:8, :] * (1.0 / N), turn_ref[8:, :] * (1.0 / N)
    turned_re = (re * cos - im * sin).reshape(64, DEV)
    turned_im = (im * cos + re * sin).reshape(64, DEV)
    plain = jnp.concatenate([turned_re, turned_im], axis=0)
    crossed = jnp.concatenate([-turned_im, turned_re], axis=0)
    data = split(jnp.concatenate([plain, crossed], axis=1))
    out = dot3(load_pair(th_ref, tl_ref), data, NT)
    lane = lax.broadcasted_iota(jnp.int32, (DEV, LANES), 1)
    for i in range(4):
        out = jnp.where(lane == NORM_LANE + i, norms[i], out)
    out_ref[...] = out


def last_kernel(got_ref, share_ref, th_ref, tl_ref, turn_ref, image_ref, found_ref):
    got = got_ref[...]
    totals = jnp.sum(got, axis=0, keepdims=True)
    norms = [jnp.sqrt(totals[:, NORM_LANE + i : NORM_LANE + i + 1]) for i in range(4)]
    lane = lax.broadcasted_iota(jnp.int32, (1, LANES), 1)
    first = norms[1] / (norms[0] * START_SCALE)
    rest = [norms[2] / norms[1], norms[3] / norms[2]]
    found_ref[...] = jnp.where(lane == 0, first, jnp.where(lane == 1, rest[0], rest[1]))
    both = dot3(split((got * share_ref[...]).T), load_pair(th_ref, tl_ref))
    by_cos, by_sin = both[:, :DEV], both[:, DEV:]
    factor = float(N) / norms[3]
    re, im = [], []
    for c in range(5):
        here, there = slice(c * 8, c * 8 + 8), slice(64 + c * 8, 72 + c * 8)
        r = by_cos[here] - by_sin[there]
        i = by_cos[there] + by_sin[here]
        cos, sin = turn_ref[c : c + 1, :] * factor, turn_ref[8 + c : 9 + c, :] * factor
        re.append(r * cos - i * sin)
        im.append(i * cos + r * sin)
    for j in range(8):
        total = re[0]
        for c in range(1, 5):
            cos = math.cos(2.0 * math.pi * (c * j % 8) / 8)
            sin = math.sin(2.0 * math.pi * (c * j % 8) / 8)
            total = total + re[c] * cos - im[c] * sin
        image_ref[:, j * 256 : (j + 1) * 256] = total


def call(kernel, outs, in_specs, flops, moved, scratch=(), limit=24):
    return pl.pallas_call(
        kernel,
        out_shape=tuple(jax.ShapeDtypeStruct(s, t) for s, t in outs),
        in_specs=in_specs,
        out_specs=tuple(VMEM for _ in outs),
        scratch_shapes=list(scratch),
        compiler_params=pltpu.CompilerParams(vmem_limit_bytes=limit * 2**20),
        cost_estimate=pl.CostEstimate(flops=flops, bytes_accessed=moved, transcendentals=0),
    )


def exchange(message):
    rows = message.shape[0]
    out = lax.all_to_all(
        message.reshape(rows, 1, LANES), AXES, 0, 0, tiled=True, axis_index_groups=[PLACES]
    )
    return out.reshape(rows, LANES)


def mirror_exchange(grid):
    return (
        lax.ppermute(grid, AXES, MIRROR),
        lax.ppermute(grid[:, :LANES], AXES, MIRROR_EDGE),
    )


def per_device(image0, interp, vis_weight, counts, tile_index):
    t = {
        k: tuple(jnp.asarray(a) for a in v) if isinstance(v, tuple) else jnp.asarray(v)
        for k, v in tables().items()
    }
    marks = jnp.concatenate(
        [tile_index.reshape(1, SLOTS), counts.reshape(1, SLOTS), jnp.zeros((6, SLOTS), jnp.int32)]
    ).astype(F32)
    pack = call(
        pack_kernel,
        [((DEV * MSG, LANES), F32), ((8, LANES), F32)],
        [VMEM, ANY] + [VMEM] * 5,
        200_000_000,
        5_000_000,
        scratch=[
            pltpu.VMEM((SLOTS, VCAP, CELLS), F32),
            pltpu.VMEM((SLOTS, LANES), F32),
            pltpu.SemaphoreType.DMA((4,)),
        ],
    )
    message, n0 = pack(
        image0,
        interp.reshape(SLOTS, VCAP, CELLS),
        vis_weight.reshape(SLOTS, VCAP),
        marks,
        *t["plain"],
        t["turn"],
    )
    got = exchange(message)
    first = call(
        first_kernel,
        [
            ((LANES, CELLS), F32),
            ((SAMPLES, CELLS), BF16),
            ((SAMPLES, CELLS), BF16),
            ((16, 256), F32),
        ],
        [VMEM] * 7,
        1_000_000_000,
        5_000_000,
    )
    grid, a_high, a_low, mask = first(
        got, *t["placed"], t["turn"], *t["eight_fwd"], t["spread"]
    )
    norms = [n0]
    follow = call(
        next_kernel,
        [((LANES, CELLS), F32), ((8, LANES), F32)],
        [VMEM] * 8,
        1_000_000_000,
        3_000_000,
    )
    for _ in range(2):
        other, edge = mirror_exchange(grid)
        grid, norm = follow(
            grid, other, edge, a_high, a_low, mask, t["flip_tile"], t["flip_cell"]
        )
        norms.append(norm)
    other, edge = mirror_exchange(grid)
    send = call(send_kernel, [((DEV, LANES), F32)], [VMEM] * 13, 300_000_000, 1_500_000)
    (message,) = send(
        grid, other, edge, *norms, t["flip_tile"], t["flip_cell"],
        *t["placed"], t["turn"], *t["eight_inv"],
    )
    got = exchange(message)
    last = call(
        last_kernel,
        [((ROWS, N), F32), ((1, LANES), F32)],
        [VMEM] * 5,
        200_000_000,
        1_500_000,
    )
    image, found = last(got, t["share"], *t["plain"], t["turn"])
    return image, found[0, :3]


def solution(mesh):
    in_specs = (
        P(AXES, None),
        P("base", "chan", None, None, None),
        P("base", "chan", None, None),
        P("base", "chan", None),
        P("base", "chan", None),
    )
    return jax.shard_map(
        per_device, mesh=mesh, in_specs=in_specs, out_specs=(P(AXES, None), P()), check_vma=False
    )
```

profile of v0, /device:TPU:1, one launch (start us, length us, event | category | flops | bytes accessed | tf_op | source)
XLA Modules:
  0.0 132.9 jit_solution(2283028964845667430)
XLA Ops:
  0.6 0.1 pad.2.clone
  0.7 0.8 copy.21
  1.5 0.8 add_convert_fusion.marks_ref
  2.3 0.0 copy-start
  2.3 1.6 %copy-done = f32[1,1,256,8,256]{4,3,2,1,0:T(8,128)S(1)} copy-done((f32[1,1,256,8,256]{4,3,2,1,0:T(8,128)S(1)}, f32[1,1,256,8,256]{4,3,2,1,0:T(8,128)}, u32[]{:S(2)}) %copy-start) | copy-done | bytes 2097176
  3.9 0.0 copy-start.1
  3.9 0.9 copy-done.1
  4.9 0.0 copy-start.3
  4.9 0.9 copy-done.3
  5.8 0.0 copy-start.7
  5.8 0.7 copy-done.7
  6.5 0.0 copy-start.11
  6.5 0.8 copy-done.11
  7.4 0.8 shard_map.185
  8.1 0.0 copy-start.5
  8.2 0.0 copy-start.6
  8.2 0.0 copy-start.15
  8.2 0.0 copy-start.16
  8.2 0.0 copy-start.17
  8.2 74.1 %all_to_all.10 = f32[4608,1,128]{2,1,0:T(1,128)S(1)} all-to-all(f32[4608,1,128]{2,1,0:T(1,128)S(1)} %bitcast.15), channel_id=1, replica_groups={{0,16,32,48,1,17,33,49,51,35,19,3,50,34,18,2,4,20,36,52,5,21,37,53,55,3..., dimensions={0} | all-to-all | bytes 4718592 | tf_op jit(solution)/shard_map/all_to_all | solution.py:373
  82.3 0.0 copy-start.10
  82.3 0.0 copy-start.12
  82.3 0.0 copy-done.5
  82.3 0.0 copy-done.6
  82.3 0.0 copy-done.15
  82.3 0.0 copy-done.16
  82.3 0.0 copy-done.17
  82.3 3.0 %shard_map.186 = (f32[128,256]{1,0:T(8,128)S(1)}, bf16[2048,256]{1,0:T(8,128)(2,1)S(1)}, bf16[2048,256]{1,0:T(8,128)(2,1)S(1)}, f32[16,256]{1,0:T(8,128)S(1)}) custom-call(f32[4608,128]{1,0:T(8,128)S(1)} %bitcast.14, bf16[256,512]{1,0:T(8,128)(2,1)S(1)} %copy-done.6, bf16[256,512]{1,0:T(8,128)(2,1)S(1)} %copy-done.5, f32[16,256]{1,0:T(8,128)S(1)} %copy-done.7, ...), custom_call_target="tpu_custom_call" | custom-call | flops 1000000000 | bytes 5000000 | tf_op jit(solution)/shard_map/pallas_call | solution.py:427
  85.3 0.1 collective-permute-start
  85.5 2.6 %collective-permute-start.1 = (f32[128,128]{1,0:T(8,128)S(1)}, f32[128,128]{1,0:T(8,128)S(1)}, u32[]{:S(2)}, u32[]{:S(2)}) collective-permute-start(f32[128,128]{1,0:T(8,128)S(1)} %slice.12), channel_id=1, source_target_pairs={{0,0},{16,8},{32,24},{48,40},{1,56},{17,9},{33,25},{49,41},{51,57}... | collective-permute-start | bytes 196616 | tf_op jit(solution)/shard_map/ppermute | solution.py:382
  88.1 3.0 %collective-permute-done.1.edge_ref = f32[128,128]{1,0:T(8,128)S(1)} collective-permute-done((f32[128,128]{1,0:T(8,128)S(1)}, f32[128,128]{1,0:T(8,128)S(1)}, u32[]{:S(2)}, u32[]{:S(2)}) %collective-permute-start.1) | collective-permute-done | bytes 65568 | tf_op jit(solution)/shard_map/ppermute | solution.py:382
  91.0 0.0 collective-permute-done.other_ref
  91.1 0.0 copy-done.10
  91.1 0.0 copy-done.12
  91.1 2.3 %shard_map.187 = (f32[128,256]{1,0:T(8,128)S(1)}, f32[8,128]{1,0:T(8,128)S(1)}) custom-call(f32[128,256]{1,0:T(8,128)S(1)} %get-tuple-element.15.own_ref, f32[128,256]{1,0:T(8,128)S(1)} %collective-permute-done.other_ref, f32[128,128]{1,0:T(8,128)S(1)} %collective-permute-done.1.edge_ref, bf16[2048,256]{1,0:T(8,128)(2,1)S(1)} %get-tuple-element.16.ah_ref, ...), custom_call_target="tpu_custom_call" | custom-call | flops 1000000000 | bytes 3000000 | tf_op jit(solution)/shard_map/pallas_call | solution.py:440
  93.3 0.0 copy-start.8
  93.4 0.0 copy-start.13
  93.4 0.0 copy-start.14
  93.4 0.1 collective-permute-start.2
  93.5 0.0 copy-start.2
  93.5 0.0 copy-start.4
  93.5 0.0 copy-start.9
  93.5 2.8 %collective-permute-start.3 = (f32[128,128]{1,0:T(8,128)S(1)}, f32[128,128]{1,0:T(8,128)S(1)}, u32[]{:S(2)}, u32[]{:S(2)}) collective-permute-start(f32[128,128]{1,0:T(8,128)S(1)} %slice.13), channel_id=1, source_target_pairs={{0,0},{16,8},{32,24},{48,40},{1,56},{17,9},{33,25},{49,41},{51,57}... | collective-permute-start | bytes 196616 | tf_op jit(solution)/shard_map/ppermute | solution.py:382
  96.4 2.9 %collective-permute-done.3.edge_ref = f32[128,128]{1,0:T(8,128)S(1)} collective-permute-done((f32[128,128]{1,0:T(8,128)S(1)}, f32[128,128]{1,0:T(8,128)S(1)}, u32[]{:S(2)}, u32[]{:S(2)}) %collective-permute-start.3) | collective-permute-done | bytes 65568 | tf_op jit(solution)/shard_map/ppermute | solution.py:382
  99.3 0.0 collective-permute-done.2.other_ref
  99.3 2.3 %shard_map.188 = (f32[128,256]{1,0:T(8,128)S(1)}, f32[8,128]{1,0:T(8,128)S(1)}) custom-call(f32[128,256]{1,0:T(8,128)S(1)} %get-tuple-element.19.own_ref, f32[128,256]{1,0:T(8,128)S(1)} %collective-permute-done.2.other_ref, f32[128,128]{1,0:T(8,128)S(1)} %collective-permute-done.3.edge_ref, bf16[2048,256]{1,0:T(8,128)(2,1)S(1)} %get-tuple-element.16.ah_ref, ...), custom_call_target="tpu_custom_call" | custom-call | flops 1000000000 | bytes 3000000 | tf_op jit(solution)/shard_map/pallas_call | solution.py:440
  101.5 0.1 collective-permute-start.4
  101.7 3.1 %collective-permute-start.5 = (f32[128,128]{1,0:T(8,128)S(1)}, f32[128,128]{1,0:T(8,128)S(1)}, u32[]{:S(2)}, u32[]{:S(2)}) collective-permute-start(f32[128,128]{1,0:T(8,128)S(1)} %slice.14), channel_id=1, source_target_pairs={{0,0},{16,8},{32,24},{48,40},{1,56},{17,9},{33,25},{49,41},{51,57}... | collective-permute-start | bytes 196616 | tf_op jit(solution)/shard_map/ppermute | solution.py:382
  104.7 2.5 %collective-permute-done.5.edge_ref = f32[128,128]{1,0:T(8,128)S(1)} collective-permute-done((f32[128,128]{1,0:T(8,128)S(1)}, f32[128,128]{1,0:T(8,128)S(1)}, u32[]{:S(2)}, u32[]{:S(2)}) %collective-permute-start.5) | collective-permute-done | bytes 65568 | tf_op jit(solution)/shard_map/ppermute | solution.py:382
  107.2 0.0 collective-permute-done.4.other_ref
  107.2 0.0 copy-done.8
  107.2 0.0 copy-done.13
  107.3 0.0 copy-done.14
  107.3 1.2 shard_map.189
  108.4 23.0 %all_to_all.11 = f32[256,1,128]{2,1,0:T(1,128)S(1)} all-to-all(f32[256,1,128]{2,1,0:T(1,128)S(1)} %bitcast.17), channel_id=1, replica_groups={{0,16,32,48,1,17,33,49,51,35,19,3,50,34,18,2,4,20,36,52,5,21,37,53,55,3..., dimensions={0} | all-to-all | bytes 262144 | tf_op jit(solution)/shard_map/all_to_all | solution.py:373
  131.4 0.0 copy-done.2
  131.4 0.0 copy-done.4
  131.4 0.0 copy-done.9
  131.4 1.0 shard_map.190
  132.4 0.5 slice_bitcast_fusion
  (4 shorter events, 0.0 us)
Async XLA Ops:
  2.3 1.6 %copy-start = (f32[1,1,256,8,256]{4,3,2,1,0:T(8,128)S(1)}, f32[1,1,256,8,256]{4,3,2,1,0:T(8,128)}, u32[]{:S(2)}) copy-start(f32[1,1,256,8,256]{4,3,2,1,0:T(8,128)} %param.19) | copy-start | bytes 6291460
  3.9 0.9 copy-start.1
  4.9 0.9 copy-start.3
  5.8 0.7 copy-start.7
  6.5 0.8 copy-start.11
  8.1 74.2 %copy-start.5 = (bf16[256,512]{1,0:T(8,128)(2,1)S(1)}, bf16[256,512]{1,0:T(8,128)(2,1)}, u32[]{:S(2)}) copy-start(bf16[256,512]{1,0:T(8,128)(2,1)} %constant.31.clone.tl_ref) | copy-start | bytes 786436
  8.2 74.2 %copy-start.6 = (bf16[256,512]{1,0:T(8,128)(2,1)S(1)}, bf16[256,512]{1,0:T(8,128)(2,1)}, u32[]{:S(2)}) copy-start(bf16[256,512]{1,0:T(8,128)(2,1)} %constant.30.clone.th_ref) | copy-start | bytes 786436
  8.2 74.2 %copy-start.15 = (bf16[256,256]{1,0:T(8,128)(2,1)S(1)}, bf16[256,256]{1,0:T(8,128)(2,1)}, u32[]{:S(2)}) copy-start(bf16[256,256]{1,0:T(8,128)(2,1)} %constant.39.clone.spread_ref) | copy-start | bytes 393220
  8.2 74.1 %copy-start.16 = (bf16[128,128]{1,0:T(8,128)(2,1)S(1)}, bf16[128,128]{1,0:T(8,128)(2,1)}, u32[]{:S(2)}) copy-start(bf16[128,128]{1,0:T(8,128)(2,1)} %constant.34.clone.el_ref) | copy-start | bytes 98308
  8.2 74.1 %copy-start.17 = (bf16[128,128]{1,0:T(8,128)(2,1)S(1)}, bf16[128,128]{1,0:T(8,128)(2,1)}, u32[]{:S(2)}) copy-start(bf16[128,128]{1,0:T(8,128)(2,1)} %constant.33.clone.eh_ref) | copy-start | bytes 98308
  82.3 8.7 %copy-start.10 = (bf16[256,256]{1,0:T(8,128)(2,1)S(1)}, bf16[256,256]{1,0:T(8,128)(2,1)}, u32[]{:S(2)}) copy-start(bf16[256,256]{1,0:T(8,128)(2,1)} %constant.38.clone.fc_ref) | copy-start | bytes 393220
  82.3 8.8 %copy-start.12 = (bf16[256,128]{1,0:T(8,128)(2,1)S(1)}, bf16[256,128]{1,0:T(8,128)(2,1)}, u32[]{:S(2)}) copy-start(bf16[256,128]{1,0:T(8,128)(2,1)} %constant.37.clone.ft_ref) | copy-start | bytes 196612
  85.3 5.7 %collective-permute-start = (f32[128,256]{1,0:T(8,128)S(1)}, f32[128,256]{1,0:T(8,128)S(1)}, u32[]{:S(2)}, u32[]{:S(2)}) collective-permute-start(f32[128,256]{1,0:T(8,128)S(1)} %get-tuple-element.15.own_ref), channel_id=1, source_target_pairs={{0,8},{16,24},{32,40},{48,56},{1,9},{17,25},{33,41},{49,57},{51,59... | collective-permute-start | bytes 393224 | tf_op jit(solution)/shard_map/ppermute | solution.py:381
  85.5 5.6 %collective-permute-start.1 = (f32[128,128]{1,0:T(8,128)S(1)}, f32[128,128]{1,0:T(8,128)S(1)}, u32[]{:S(2)}, u32[]{:S(2)}) collective-permute-start(f32[128,128]{1,0:T(8,128)S(1)} %slice.12), channel_id=1, source_target_pairs={{0,0},{16,8},{32,24},{48,40},{1,56},{17,9},{33,25},{49,41},{51,57}... | collective-permute-start | bytes 196616 | tf_op jit(solution)/shard_map/ppermute | solution.py:382
  93.3 13.9 %copy-start.8 = (f32[16,256]{1,0:T(8,128)S(1)}, f32[16,256]{1,0:T(8,128)}, u32[]{:S(2)}) copy-start(f32[16,256]{1,0:T(8,128)} %constant.32.clone.turn_ref) | copy-start | bytes 49156
  93.4 13.9 %copy-start.13 = (bf16[128,128]{1,0:T(8,128)(2,1)S(1)}, bf16[128,128]{1,0:T(8,128)(2,1)}, u32[]{:S(2)}) copy-start(bf16[128,128]{1,0:T(8,128)(2,1)} %constant.36.clone.el_ref) | copy-start | bytes 98308
  93.4 13.9 %copy-start.14 = (bf16[128,128]{1,0:T(8,128)(2,1)S(1)}, bf16[128,128]{1,0:T(8,128)(2,1)}, u32[]{:S(2)}) copy-start(bf16[128,128]{1,0:T(8,128)(2,1)} %constant.35.clone.eh_ref) | copy-start | bytes 98308
  93.4 5.9 %collective-permute-start.2 = (f32[128,256]{1,0:T(8,128)S(1)}, f32[128,256]{1,0:T(8,128)S(1)}, u32[]{:S(2)}, u32[]{:S(2)}) collective-permute-start(f32[128,256]{1,0:T(8,128)S(1)} %get-tuple-element.19.own_ref), channel_id=1, source_target_pairs={{0,8},{16,24},{32,40},{48,56},{1,9},{17,25},{33,41},{49,57},{51,59... | collective-permute-start | bytes 393224 | tf_op jit(solution)/shard_map/ppermute | solution.py:381
  93.5 37.9 %copy-start.2 = (bf16[256,512]{1,0:T(8,128)(2,1)S(1)}, bf16[256,512]{1,0:T(8,128)(2,1)}, u32[]{:S(2)}) copy-start(bf16[256,512]{1,0:T(8,128)(2,1)} %constant.29.clone.tl_ref) | copy-start | bytes 786436
  93.5 37.9 %copy-start.4 = (bf16[256,512]{1,0:T(8,128)(2,1)S(1)}, bf16[256,512]{1,0:T(8,128)(2,1)}, u32[]{:S(2)}) copy-start(bf16[256,512]{1,0:T(8,128)(2,1)} %constant.28.clone.th_ref) | copy-start | bytes 786436
  93.5 37.9 %copy-start.9 = (f32[256,128]{1,0:T(8,128)S(1)}, f32[256,128]{1,0:T(8,128)}, u32[]{:S(2)}) copy-start(f32[256,128]{1,0:T(8,128)} %constant.40.clone.share_ref) | copy-start | bytes 393220
  93.5 5.7 %collective-permute-start.3 = (f32[128,128]{1,0:T(8,128)S(1)}, f32[128,128]{1,0:T(8,128)S(1)}, u32[]{:S(2)}, u32[]{:S(2)}) collective-permute-start(f32[128,128]{1,0:T(8,128)S(1)} %slice.13), channel_id=1, source_target_pairs={{0,0},{16,8},{32,24},{48,40},{1,56},{17,9},{33,25},{49,41},{51,57}... | collective-permute-start | bytes 196616 | tf_op jit(solution)/shard_map/ppermute | solution.py:382
  101.5 5.7 %collective-permute-start.4 = (f32[128,256]{1,0:T(8,128)S(1)}, f32[128,256]{1,0:T(8,128)S(1)}, u32[]{:S(2)}, u32[]{:S(2)}) collective-permute-start(f32[128,256]{1,0:T(8,128)S(1)} %get-tuple-element.20.own_ref), channel_id=1, source_target_pairs={{0,8},{16,24},{32,40},{48,56},{1,9},{17,25},{33,41},{49,57},{51,59... | collective-permute-start | bytes 393224 | tf_op jit(solution)/shard_map/ppermute | solution.py:381
  101.7 5.6 %collective-permute-start.5 = (f32[128,128]{1,0:T(8,128)S(1)}, f32[128,128]{1,0:T(8,128)S(1)}, u32[]{:S(2)}, u32[]{:S(2)}) collective-permute-start(f32[128,128]{1,0:T(8,128)S(1)} %slice.14), channel_id=1, source_target_pairs={{0,0},{16,8},{32,24},{48,40},{1,56},{17,9},{33,25},{49,41},{51,57}... | collective-permute-start | bytes 196616 | tf_op jit(solution)/shard_map/ppermute | solution.py:382
where the time goes:
time: 133 us
  blocking collectives  97.1 us (73%)
  Pallas kernels  10.5 us (8%)
  starting transfers between devices  8.79 us (7%)
  waiting for transfers between devices  8.36 us (6%)
  local copies, waits for them, and re-layouts  6.55 us (5%)
    all_to_all x2, blocking collectives, exchange(): lax.all_to_all(message.reshape(rows, 1, LANES), AXES, 0, 0, tiled=True, a...  97.1 us
    ppermute x3, starting transfers between devices, mirror_exchange(): lax.ppermute(grid[:, :LANES], AXES, MIRROR_EDGE)  8.51 us
    ppermute x3, waiting for transfers between devices, mirror_exchange(): lax.ppermute(grid[:, :LANES], AXES, MIRROR_EDGE)  8.35 us
    unnamed x37, local copies, waits for them, and re-layouts  5.95 us
    pallas_call x2, Pallas kernels, per_device(): follow(grid, other, edge, a_high, a_low, mask, t['flip_tile'], t['flip_ce...  4.56 us
    pallas_call x1, Pallas kernels, per_device(): first(got, *t['placed'], t['turn'], *t['eight_fwd'], t['spread'])  2.99 us
  transfers between devices with their start and end apart: 6, of which 3 were waited for; matrix products, arithmetic and copies ran while one was open for 0% of the time, Pallas kernels for 0%

commit v1 on v0

--- a/solution.py
+++ b/solution.py
@@ -23,10 +23,11 @@
 GROUP = 4
 START_SCALE = 2.0**-11
 NORM_LANE = 40
+PACK_LIMIT = 64_200_000
 F32 = jnp.float32
 BF16 = jnp.bfloat16
 VMEM = pl.BlockSpec(memory_space=pltpu.VMEM)
-ANY = pl.BlockSpec(memory_space=pl.ANY)
+HBM = pl.BlockSpec(memory_space=pltpu.HBM)
 
 
 def chip_path():
@@ -115,7 +116,9 @@
 
 def dot3(a, b, dims=((1,), (0,))):
     (ah, al), (bh, bl) = a, b
-    return dot(ah, bh, dims) + (dot(ah, bl, dims) + dot(al, bh, dims))
+    rows = ah.shape[0]
+    both = dot(jnp.concatenate([ah, al], axis=0), bh, dims)
+    return both[:rows] + (both[rows:] + dot(ah, bl, dims))
 
 
 NT = ((1,), (1,))
@@ -163,13 +166,13 @@
     return total
 
 
-def apply_matrix(spectrum, ah_ref, al_ref, mask_ref):
+def apply_matrix(spectrum, samples, mask_ref):
     parts = split(spectrum)
     row = lax.broadcasted_iota(jnp.int32, (LANES, 256), 0)
     tile = (row % 8 * 8 + row // 8 % 8).astype(F32)
     total = None
     for m in range(SAMPLES // 256):
-        a = (ah_ref[pl.ds(m * 256, 256), :], al_ref[pl.ds(m * 256, 256), :])
+        a = samples(m)
         seen = dot3(parts, a, NT)
         weight = mask_ref[m : m + 1, :]
         wanted = mask_ref[8 + m : 9 + m, :]
@@ -179,32 +182,61 @@
     return total
 
 
+def stored_samples(ah_ref, al_ref):
+    return lambda m: (ah_ref[pl.ds(m * 256, 256), :], al_ref[pl.ds(m * 256, 256), :])
+
+
+def pack_edge(grid):
+    chunk = lax.broadcasted_iota(jnp.int32, (32, LANES), 1) // 32
+    made = grid[:32, :LANES]
+    for i in range(1, 4):
+        moved = pltpu.roll(grid[i * 32 : i * 32 + 32, :LANES], i * 32, 1)
+        made = jnp.where(chunk == i, moved, made)
+    return made
+
+
+def unpack_edge(edge):
+    return jnp.concatenate(
+        [edge] + [pltpu.roll(edge, LANES - i * 32, 1) for i in range(1, 4)], axis=0
+    )
+
+
 def mirrored(own_ref, other_ref, edge_ref, flip_tile_ref, flip_cell_ref):
     lane = lax.broadcasted_iota(jnp.int32, (LANES, CELLS), 1)
     other = other_ref[...]
-    edge = jnp.concatenate([edge_ref[...], other[:, LANES:]], axis=1)
+    edge = jnp.concatenate([unpack_edge(edge_ref[...]), other[:, LANES:]], axis=1)
     other = jnp.where(lane < 32, edge, other)
     high, low = split(other)
     flips = flip_tile_ref[...]
-    turned = dot(flips, high) + dot(flips, low)
+    turned = dot(jnp.concatenate([flips, flips], axis=1), jnp.concatenate([high, low], axis=0))
     turned = jnp.where(lane % 32 == 0, turned[LANES:], turned[:LANES])
     high, low = split(turned)
     flip = flip_cell_ref[...]
-    return 0.5 * (own_ref[...] + (dot(high, flip) + dot(low, flip)))
-
-
-def pack_kernel(image_ref, interp_ref, weight_ref, marks_ref, th_ref, tl_ref, turn_ref,
-                out_ref, norm_ref, held, extra, sems):
-    pieces = 4
+    turned = dot(jnp.concatenate([high, low], axis=0), flip)
+    return 0.5 * (own_ref[...] + (turned[:LANES] + turned[LANES:]))
+
+
+def pack_kernel(image_hbm, interp_hbm, weight_hbm, index_hbm, counts_hbm, th_hbm, tl_hbm, turn_hbm,
+                out_hbm, norm_ref, out_ref, image_ref, held, weight_ref, index_ref, counts_ref,
+                th_ref, tl_ref, turn_ref, sems):
+    pieces = 8
     size = SLOTS // pieces
+    pairs = [
+        (image_hbm, image_ref), (turn_hbm, turn_ref), (th_hbm, th_ref), (tl_hbm, tl_ref),
+        (index_hbm, index_ref), (counts_hbm, counts_ref), (weight_hbm, weight_ref),
+    ]
+    pairs += [
+        (interp_hbm.at[pl.ds(i * size, size)], held.at[pl.ds(i * size, size)])
+        for i in range(pieces)
+    ]
     copies = [
-        pltpu.make_async_copy(
-            interp_ref.at[pl.ds(i * size, size)], held.at[pl.ds(i * size, size)], sems.at[i]
-        )
-        for i in range(pieces)
+        pltpu.make_async_copy(source, target, sems.at[i])
+        for i, (source, target) in enumerate(pairs)
     ]
     for copy in copies:
         copy.start()
+    copies[0].wait()
+    copies[1].wait()
     image = image_ref[...]
     x = [image[:, q * 256 : (q + 1) * 256] for q in range(8)]
     squares = None
@@ -229,14 +261,22 @@
     plain = jnp.concatenate(turned_re + turned_im, axis=0)
     crossed = jnp.concatenate(turned_im + [-v for v in turned_re], axis=0)
     data = split(jnp.concatenate([plain, crossed], axis=1))
+    copies[2].wait()
+    copies[3].wait()
     columns = dot3(load_pair(th_ref, tl_ref), data, NT)
     out_ref[pl.ds(16, DEV, stride=MSG), :] = columns
+    for i in (4, 5, 6):
+        copies[i].wait()
     marks = jnp.concatenate(
-        [jnp.zeros((8, SLOTS), F32), marks_ref[...], jnp.zeros((LANES - 16, SLOTS), F32)], axis=0
-    )
-    extra[...] = marks.T
-    extra[:, :VCAP] = weight_ref[...]
-    out_ref[pl.ds(17, DEV, stride=MSG), :] = extra[...]
+        [
+            weight_ref[...],
+            index_ref[...].astype(F32),
+            counts_ref[...].astype(F32),
+            jnp.zeros((LANES - 10, SLOTS), F32),
+        ],
+        axis=0,
+    )
+    out_ref[pl.ds(17, DEV, stride=MSG), :] = marks.T
 
     def move(group, carry):
         base = pl.multiple_of(group * (GROUP * MSG), 8)
@@ -248,30 +288,33 @@
         return carry
 
     groups = SLOTS // GROUP // pieces
+    rows = size * MSG
+    sent = []
     for i in range(pieces):
-        copies[i].wait()
+        copies[7 + i].wait()
         lax.fori_loop(i * groups, (i + 1) * groups, move, 0, unroll=2)
+        part = pl.ds(i * rows, rows)
+        sent.append(
+            pltpu.make_async_copy(out_ref.at[part], out_hbm.at[part], sems.at[15 + i])
+        )
+        sent[-1].start()
+    for copy in sent:
+        copy.wait()
 
 
 def first_kernel(got_ref, th_ref, tl_ref, turn_ref, eh_ref, el_ref, spread_ref,
-                 out_ref, ah_ref, al_ref, mask_ref):
-    def unpack(group, carry):
-        base = pl.multiple_of(group * (GROUP * MSG), 8)
-        for pair in range(GROUP // 2):
-            rows = []
-            for m in (2 * pair, 2 * pair + 1):
-                rows.append(
-                    jnp.concatenate(
-                        [got_ref[pl.ds(base + m * MSG + t * 8, 8), :] for t in range(2)], axis=1
-                    )
-                )
-            high, low = split(jnp.concatenate(rows, axis=0))
-            start = pl.multiple_of(group * 32 + pair * 16, 16)
-            ah_ref[pl.ds(start, 16), :] = high
-            al_ref[pl.ds(start, 16), :] = low
-        return carry
-
-    lax.fori_loop(0, SLOTS // GROUP, unpack, 0, unroll=2)
+                 out_ref, edge_ref, ah_ref, al_ref, mask_ref):
+    def samples(m):
+        slots = [
+            jnp.concatenate(
+                [got_ref[pl.ds(slot * MSG + t * 8, 8), :] for t in range(2)], axis=1
+            )
+            for slot in range(m * 32, m * 32 + 32)
+        ]
+        high, low = split(jnp.concatenate(slots, axis=0))
+        ah_ref[pl.ds(m * 256, 256), :] = high
+        al_ref[pl.ds(m * 256, 256), :] = low
+        return high, low
 
     marks = got_ref[pl.ds(17, DEV, stride=MSG), :].T[:16]
     chunk = lax.broadcasted_iota(jnp.int32, (16, SLOTS), 1) // 32
@@ -298,14 +341,18 @@
     cos, sin = turn_ref[:8, :] * scale, turn_ref[8:, :] * scale
     turned = jnp.concatenate([re * cos + im * sin, im * cos - re * sin], axis=0)
     spectrum = dot3(load_pair(eh_ref, el_ref), split(turned.reshape(LANES, DEV)))
-    out_ref[...] = apply_matrix(swap_chunks(spectrum), ah_ref, al_ref, mask_ref)
+    grid = apply_matrix(swap_chunks(spectrum), samples, mask_ref)
+    out_ref[...] = grid
+    edge_ref[...] = pack_edge(grid)
 
 
 def next_kernel(own_ref, other_ref, edge_ref, ah_ref, al_ref, mask_ref, ft_ref, fc_ref,
-                out_ref, norm_ref):
+                out_ref, edge_out_ref, norm_ref):
     spectrum = mirrored(own_ref, other_ref, edge_ref, ft_ref, fc_ref)
     norm_ref[...] = fold(spectrum)
-    out_ref[...] = apply_matrix(spectrum, ah_ref, al_ref, mask_ref)
+    grid = apply_matrix(spectrum, stored_samples(ah_ref, al_ref), mask_ref)
+    out_ref[...] = grid
+    edge_out_ref[...] = pack_edge(grid)
 
 
 def send_kernel(own_ref, other_ref, edge_ref, n0_ref, n1_ref, n2_ref, ft_ref, fc_ref,
@@ -332,9 +379,9 @@
     got = got_ref[...]
     totals = jnp.sum(got, axis=0, keepdims=True)
     norms = [jnp.sqrt(totals[:, NORM_LANE + i : NORM_LANE + i + 1]) for i in range(4)]
-    lane = lax.broadcasted_iota(jnp.int32, (1, LANES), 1)
     first = norms[1] / (norms[0] * START_SCALE)
     rest = [norms[2] / norms[1], norms[3] / norms[2]]
+    lane = lax.broadcasted_iota(jnp.int32, (1, 3), 1)
     found_ref[...] = jnp.where(lane == 0, first, jnp.where(lane == 1, rest[0], rest[1]))
     both = dot3(split((got * share_ref[...]).T), load_pair(th_ref, tl_ref))
     by_cos, by_sin = both[:, :DEV], both[:, DEV:]
@@ -356,14 +403,14 @@
         image_ref[:, j * 256 : (j + 1) * 256] = total
 
 
-def call(kernel, outs, in_specs, flops, moved, scratch=(), limit=24):
+def call(kernel, outs, in_specs, flops, moved, scratch=(), limit=24 * 2**20, out_specs=None):
     return pl.pallas_call(
         kernel,
         out_shape=tuple(jax.ShapeDtypeStruct(s, t) for s, t in outs),
         in_specs=in_specs,
-        out_specs=tuple(VMEM for _ in outs),
+        out_specs=out_specs or tuple(VMEM for _ in outs),
         scratch_shapes=list(scratch),
-        compiler_params=pltpu.CompilerParams(vmem_limit_bytes=limit * 2**20),
+        compiler_params=pltpu.CompilerParams(vmem_limit_bytes=limit),
         cost_estimate=pl.CostEstimate(flops=flops, bytes_accessed=moved, transcendentals=0),
     )
 
@@ -376,11 +423,10 @@
     return out.reshape(rows, LANES)
 
 
-def mirror_exchange(grid):
-    return (
-        lax.ppermute(grid, AXES, MIRROR),
-        lax.ppermute(grid[:, :LANES], AXES, MIRROR_EDGE),
-    )
+def mirror_exchange(grid, edge):
+    edge = lax.ppermute(edge, AXES, MIRROR_EDGE)
+    other = lax.ppermute(grid, AXES, MIRROR)
+    return grid, other, edge
 
 
 def per_device(image0, interp, vis_weight, counts, tile_index):
@@ -388,26 +434,33 @@
         k: tuple(jnp.asarray(a) for a in v) if isinstance(v, tuple) else jnp.asarray(v)
         for k, v in tables().items()
     }
-    marks = jnp.concatenate(
-        [tile_index.reshape(1, SLOTS), counts.reshape(1, SLOTS), jnp.zeros((6, SLOTS), jnp.int32)]
-    ).astype(F32)
     pack = call(
         pack_kernel,
         [((DEV * MSG, LANES), F32), ((8, LANES), F32)],
-        [VMEM, ANY] + [VMEM] * 5,
+        [HBM] * 8,
         200_000_000,
         5_000_000,
         scratch=[
+            pltpu.VMEM((DEV * MSG, LANES), F32),
+            pltpu.VMEM((ROWS, N), F32),
             pltpu.VMEM((SLOTS, VCAP, CELLS), F32),
-            pltpu.VMEM((SLOTS, LANES), F32),
-            pltpu.SemaphoreType.DMA((4,)),
+            pltpu.VMEM((VCAP, SLOTS), F32),
+            pltpu.VMEM((1, SLOTS), jnp.int32),
+            pltpu.VMEM((1, SLOTS), jnp.int32),
+            pltpu.VMEM((DEV, 2 * DEV), BF16),
+            pltpu.VMEM((DEV, 2 * DEV), BF16),
+            pltpu.VMEM((16, DEV), F32),
+            pltpu.SemaphoreType.DMA((23,)),
         ],
+        limit=PACK_LIMIT,
+        out_specs=(HBM, VMEM),
     )
     message, n0 = pack(
         image0,
         interp.reshape(SLOTS, VCAP, CELLS),
-        vis_weight.reshape(SLOTS, VCAP),
-        marks,
+        vis_weight.reshape(SLOTS, VCAP).T,
+        tile_index.reshape(1, SLOTS),
+        counts.reshape(1, SLOTS),
         *t["plain"],
         t["turn"],
     )
@@ -416,6 +469,7 @@
         first_kernel,
         [
             ((LANES, CELLS), F32),
+            ((32, LANES), F32),
             ((SAMPLES, CELLS), BF16),
             ((SAMPLES, CELLS), BF16),
             ((16, 256), F32),
@@ -424,39 +478,39 @@
         1_000_000_000,
         5_000_000,
     )
-    grid, a_high, a_low, mask = first(
+    grid, edge, a_high, a_low, mask = first(
         got, *t["placed"], t["turn"], *t["eight_fwd"], t["spread"]
     )
     norms = [n0]
     follow = call(
         next_kernel,
-        [((LANES, CELLS), F32), ((8, LANES), F32)],
+        [((LANES, CELLS), F32), ((32, LANES), F32), ((8, LANES), F32)],
         [VMEM] * 8,
         1_000_000_000,
         3_000_000,
     )
     for _ in range(2):
-        other, edge = mirror_exchange(grid)
-        grid, norm = follow(
-            grid, other, edge, a_high, a_low, mask, t["flip_tile"], t["flip_cell"]
+        blocks = mirror_exchange(grid, edge)
+        grid, edge, norm = follow(
+            *blocks, a_high, a_low, mask, t["flip_tile"], t["flip_cell"]
         )
         norms.append(norm)
-    other, edge = mirror_exchange(grid)
+    blocks = mirror_exchange(grid, edge)
     send = call(send_kernel, [((DEV, LANES), F32)], [VMEM] * 13, 300_000_000, 1_500_000)
     (message,) = send(
-        grid, other, edge, *norms, t["flip_tile"], t["flip_cell"],
+        *blocks, *norms, t["flip_tile"], t["flip_cell"],
         *t["placed"], t["turn"], *t["eight_inv"],
     )
     got = exchange(message)
     last = call(
         last_kernel,
-        [((ROWS, N), F32), ((1, LANES), F32)],
+        [((ROWS, N), F32), ((1, 3), F32)],
         [VMEM] * 5,
         200_000_000,
         1_500_000,
     )
     image, found = last(got, t["share"], *t["plain"], t["turn"])
-    return image, found[0, :3]
+    return image, found.reshape(3)
 
 
 def solution(mesh):

time: 133 us -> 126 us (0.947)
  local copies, waits for them, and re-layouts: 6.55 us -> 0.09 us
  waiting for transfers between devices: 8.36 us -> 6.77 us
  Pallas kernels: 10.5 us -> 11.9 us
    unnamed x37 -> x28, local copies, waits for them, and re-layouts: 5.95 us -> 0.09 us
    pallas_call x1, Pallas kernels: 0.77 us -> 3.81 us  [per_device(): pack(image0, interp.reshape(SLOTS, VCAP, CELLS), vis_weight.reshape(SLOTS...]
    ppermute x6, waiting for transfers between devices: 8.36 us -> 6.77 us  [the longest x3 6.77 us: mirror_exchange(): edge = lax.ppermute(edge, AXES, MIRROR_EDGE)]
where the time goes in v1:
time: 126 us
  blocking collectives  97.3 us (77%)
  Pallas kernels  11.9 us (9%)
  starting transfers between devices  8.79 us (7%)
  waiting for transfers between devices  6.77 us (5%)
    all_to_all x2, blocking collectives, exchange(): lax.all_to_all(message.reshape(rows, 1, LANES), AXES, 0, 0, tiled=True, a...  97.3 us
    ppermute x3, starting transfers between devices, mirror_exchange(): edge = lax.ppermute(edge, AXES, MIRROR_EDGE)  8.51 us
    ppermute x3, waiting for transfers between devices, mirror_exchange(): edge = lax.ppermute(edge, AXES, MIRROR_EDGE)  6.77 us
    pallas_call x1, Pallas kernels, per_device(): pack(image0, interp.reshape(SLOTS, VCAP, CELLS), vis_weight.reshape(SLOTS...  3.81 us
    pallas_call x2, Pallas kernels, per_device(): follow(*blocks, a_high, a_low, mask, t['flip_tile'], t['flip_cell'])  3.73 us
  transfers between devices with their start and end apart: 6, of which 3 were waited for; matrix products, arithmetic and copies ran while one was open for 0% of the time, Pallas kernels for 0%

profile of v1, /device:TPU:1, one launch (start us, length us, event | category | flops | bytes accessed | tf_op | source)
XLA Modules:
  0.0 125.7 jit_solution(4113978890304851817)
XLA Ops:
  0.6 3.8 %shard_map.185 = (f32[4608,128]{1,0:T(8,128)}, f32[8,128]{1,0:T(8,128)}) custom-call(f32[8,2048]{1,0:T(8,128)} %image_hbm.1, f32[256,8,256]{2,1,0:T(8,128)} %bitcast.19, f32[8,256]{1,0:T(8,128)} %bitcast.20, s32[1,256]{1,0:T(1,128)} %bitcast.21, s32[1,256]{1,0:T(1,128)} %bitcast.22, bf16[256,512]{1,0:T(8,128)(2,1)} %constant.26.clone.th_hbm.th_ref, ...), custom_call_target="tpu_custom_call" | custom-call | flops 200000000 | bytes 5000000 | tf_op jit(solution)/shard_map/pallas_call | solution.py:458
  4.5 0.0 copy-start.2
  4.5 0.0 copy-start.3
  4.5 0.0 copy-start.4
  4.5 0.0 copy-start.11
  4.5 0.0 copy-start.12
  4.5 0.0 copy-start.13
  4.5 74.3 %all_to_all.10 = f32[4608,1,128]{2,1,0:T(1,128)S(1)} all-to-all(f32[4608,1,128]{2,1,0:T(1,128)} %bitcast.18), channel_id=1, replica_groups={{0,16,32,48,1,17,33,49,51,35,19,3,50,34,18,2,4,20,36,52,5,21,37,53,55,3..., dimensions={0} | all-to-all | bytes 4718592 | tf_op jit(solution)/shard_map/all_to_all | solution.py:420
  78.8 0.0 copy-start.6
  78.8 0.0 copy-start.7
  78.8 0.0 copy-done.2
  78.8 0.0 copy-done.3
  78.9 0.0 copy-done.4
  78.9 0.0 copy-done.11
  78.9 0.0 copy-done.12
  78.9 0.0 copy-done.13
  78.9 2.2 %shard_map.186 = (f32[128,256]{1,0:T(8,128)S(1)}, f32[32,128]{1,0:T(8,128)S(1)}, bf16[2048,256]{1,0:T(8,128)(2,1)S(1)}, bf16[2048,256]{1,0:T(8,128)(2,1)S(1)}, f32[16,256]{1,0:T(8,128)S(1)}) custom-call(f32[4608,128]{1,0:T(8,128)S(1)} %bitcast.15, bf16[256,512]{1,0:T(8,128)(2,1)S(1)} %copy-done.3, bf16[256,512]{1,0:T(8,128)(2,1)S(1)} %copy-done.2, ...), custom_call_target="tpu_custom_call" | custom-call | flops 1000000000 | bytes 5000000 | tf_op jit(solution)/shard_map/pallas_call | solution.py:481
  81.1 0.1 collective-permute-start
  81.2 2.6 %collective-permute-start.1 = (f32[32,128]{1,0:T(8,128)S(1)}, f32[32,128]{1,0:T(8,128)S(1)}, u32[]{:S(2)}, u32[]{:S(2)}) collective-permute-start(f32[32,128]{1,0:T(8,128)S(1)} %get-tuple-element.19), channel_id=1, source_target_pairs={{0,0},{16,8},{32,24},{48,40},{1,56},{17,9},{33,25},{49,41},{51,57}... | collective-permute-start | bytes 49160 | tf_op jit(solution)/shard_map/ppermute | solution.py:427
  83.8 2.4 %collective-permute-done.1.edge_ref = f32[32,128]{1,0:T(8,128)S(1)} collective-permute-done((f32[32,128]{1,0:T(8,128)S(1)}, f32[32,128]{1,0:T(8,128)S(1)}, u32[]{:S(2)}, u32[]{:S(2)}) %collective-permute-start.1) | collective-permute-done | bytes 16416 | tf_op jit(solution)/shard_map/ppermute | solution.py:427
  86.2 0.0 collective-permute-done.other_ref
  86.2 0.0 copy-done.6
  86.2 0.0 copy-done.7
  86.2 1.9 %shard_map.187 = (f32[128,256]{1,0:T(8,128)S(1)}, f32[32,128]{1,0:T(8,128)S(1)}, f32[8,128]{1,0:T(8,128)S(1)}) custom-call(f32[128,256]{1,0:T(8,128)S(1)} %get-tuple-element.18.own_ref, f32[128,256]{1,0:T(8,128)S(1)} %collective-permute-done.other_ref, f32[32,128]{1,0:T(8,128)S(1)} %collective-permute-done.1.edge_ref, ...), custom_call_target="tpu_custom_call" | custom-call | flops 1000000000 | bytes 3000000 | tf_op jit(solution)/shard_map/pallas_call | solution.py:494
  88.1 0.0 copy-start.8
  88.1 0.0 copy-start.9
  88.1 0.0 copy-start.10
  88.1 0.1 collective-permute-start.2
  88.2 0.0 copy-start
  88.3 0.0 copy-start.1
  88.3 0.0 copy-start.5
  88.3 2.8 %collective-permute-start.3 = (f32[32,128]{1,0:T(8,128)S(1)}, f32[32,128]{1,0:T(8,128)S(1)}, u32[]{:S(2)}, u32[]{:S(2)}) collective-permute-start(f32[32,128]{1,0:T(8,128)S(1)} %get-tuple-element.24), channel_id=1, source_target_pairs={{0,0},{16,8},{32,24},{48,40},{1,56},{17,9},{33,25},{49,41},{51,57}... | collective-permute-start | bytes 49160 | tf_op jit(solution)/shard_map/ppermute | solution.py:427
  91.1 2.4 %collective-permute-done.3.edge_ref = f32[32,128]{1,0:T(8,128)S(1)} collective-permute-done((f32[32,128]{1,0:T(8,128)S(1)}, f32[32,128]{1,0:T(8,128)S(1)}, u32[]{:S(2)}, u32[]{:S(2)}) %collective-permute-start.3) | collective-permute-done | bytes 16416 | tf_op jit(solution)/shard_map/ppermute | solution.py:427
  93.5 0.0 collective-permute-done.2.other_ref
  93.5 1.9 %shard_map.188 = (f32[128,256]{1,0:T(8,128)S(1)}, f32[32,128]{1,0:T(8,128)S(1)}, f32[8,128]{1,0:T(8,128)S(1)}) custom-call(f32[128,256]{1,0:T(8,128)S(1)} %get-tuple-element.23.own_ref, f32[128,256]{1,0:T(8,128)S(1)} %collective-permute-done.2.other_ref, f32[32,128]{1,0:T(8,128)S(1)} %collective-permute-done.3.edge_ref, ...), custom_call_target="tpu_custom_call" | custom-call | flops 1000000000 | bytes 3000000 | tf_op jit(solution)/shard_map/pallas_call | solution.py:494
  95.3 0.1 collective-permute-start.4
  95.4 3.1 %collective-permute-start.5 = (f32[32,128]{1,0:T(8,128)S(1)}, f32[32,128]{1,0:T(8,128)S(1)}, u32[]{:S(2)}, u32[]{:S(2)}) collective-permute-start(f32[32,128]{1,0:T(8,128)S(1)} %get-tuple-element.26), channel_id=1, source_target_pairs={{0,0},{16,8},{32,24},{48,40},{1,56},{17,9},{33,25},{49,41},{51,57}... | collective-permute-start | bytes 49160 | tf_op jit(solution)/shard_map/ppermute | solution.py:427
  98.5 2.0 %collective-permute-done.5.edge_ref = f32[32,128]{1,0:T(8,128)S(1)} collective-permute-done((f32[32,128]{1,0:T(8,128)S(1)}, f32[32,128]{1,0:T(8,128)S(1)}, u32[]{:S(2)}, u32[]{:S(2)}) %collective-permute-start.5) | collective-permute-done | bytes 16416 | tf_op jit(solution)/shard_map/ppermute | solution.py:427
  100.5 0.0 collective-permute-done.4.other_ref
  100.5 0.0 copy-done.8
  100.5 0.0 copy-done.9
  100.5 0.0 copy-done.10
  100.5 1.2 shard_map.189
  101.8 23.0 %all_to_all.11 = f32[256,1,128]{2,1,0:T(1,128)S(1)} all-to-all(f32[256,1,128]{2,1,0:T(1,128)S(1)} %bitcast.16), channel_id=1, replica_groups={{0,16,32,48,1,17,33,49,51,35,19,3,50,34,18,2,4,20,36,52,5,21,37,53,55,3..., dimensions={0} | all-to-all | bytes 262144 | tf_op jit(solution)/shard_map/all_to_all | solution.py:420
  124.7 0.0 copy-done
  124.7 0.0 copy-done.1
  124.7 0.0 copy-done.5
  124.7 1.0 shard_map.190
Async XLA Ops:
  4.5 74.4 %copy-start.2 = (bf16[256,512]{1,0:T(8,128)(2,1)S(1)}, bf16[256,512]{1,0:T(8,128)(2,1)}, u32[]{:S(2)}) copy-start(bf16[256,512]{1,0:T(8,128)(2,1)} %constant.29.clone.tl_ref) | copy-start | bytes 786436
  4.5 74.4 %copy-start.3 = (bf16[256,512]{1,0:T(8,128)(2,1)S(1)}, bf16[256,512]{1,0:T(8,128)(2,1)}, u32[]{:S(2)}) copy-start(bf16[256,512]{1,0:T(8,128)(2,1)} %constant.28.clone.th_ref) | copy-start | bytes 786436
  4.5 74.4 %copy-start.4 = (f32[16,256]{1,0:T(8,128)S(1)}, f32[16,256]{1,0:T(8,128)}, u32[]{:S(2)}) copy-start(f32[16,256]{1,0:T(8,128)} %constant.30.clone.turn_hbm.turn_ref) | copy-start | bytes 49156
  4.5 74.4 %copy-start.11 = (bf16[256,256]{1,0:T(8,128)(2,1)S(1)}, bf16[256,256]{1,0:T(8,128)(2,1)}, u32[]{:S(2)}) copy-start(bf16[256,256]{1,0:T(8,128)(2,1)} %constant.37.clone.spread_ref) | copy-start | bytes 393220
  4.5 74.4 %copy-start.12 = (bf16[128,128]{1,0:T(8,128)(2,1)S(1)}, bf16[128,128]{1,0:T(8,128)(2,1)}, u32[]{:S(2)}) copy-start(bf16[128,128]{1,0:T(8,128)(2,1)} %constant.32.clone.el_ref) | copy-start | bytes 98308
  4.5 74.4 %copy-start.13 = (bf16[128,128]{1,0:T(8,128)(2,1)S(1)}, bf16[128,128]{1,0:T(8,128)(2,1)}, u32[]{:S(2)}) copy-start(bf16[128,128]{1,0:T(8,128)(2,1)} %constant.31.clone.eh_ref) | copy-start | bytes 98308
  78.8 7.4 %copy-start.6 = (bf16[256,256]{1,0:T(8,128)(2,1)S(1)}, bf16[256,256]{1,0:T(8,128)(2,1)}, u32[]{:S(2)}) copy-start(bf16[256,256]{1,0:T(8,128)(2,1)} %constant.36.clone.fc_ref) | copy-start | bytes 393220
  78.8 7.4 %copy-start.7 = (bf16[256,128]{1,0:T(8,128)(2,1)S(1)}, bf16[256,128]{1,0:T(8,128)(2,1)}, u32[]{:S(2)}) copy-start(bf16[256,128]{1,0:T(8,128)(2,1)} %constant.35.clone.ft_ref) | copy-start | bytes 196612
  81.1 5.2 %collective-permute-start = (f32[128,256]{1,0:T(8,128)S(1)}, f32[128,256]{1,0:T(8,128)S(1)}, u32[]{:S(2)}, u32[]{:S(2)}) collective-permute-start(f32[128,256]{1,0:T(8,128)S(1)} %get-tuple-element.18.own_ref), channel_id=1, source_target_pairs={{0,8},{16,24},{32,40},{48,56},{1,9},{17,25},{33,41},{49,57},{51,59... | collective-permute-start | bytes 393224 | tf_op jit(solution)/shard_map/ppermute | solution.py:428
  81.2 5.1 %collective-permute-start.1 = (f32[32,128]{1,0:T(8,128)S(1)}, f32[32,128]{1,0:T(8,128)S(1)}, u32[]{:S(2)}, u32[]{:S(2)}) collective-permute-start(f32[32,128]{1,0:T(8,128)S(1)} %get-tuple-element.19), channel_id=1, source_target_pairs={{0,0},{16,8},{32,24},{48,40},{1,56},{17,9},{33,25},{49,41},{51,57}... | collective-permute-start | bytes 49160 | tf_op jit(solution)/shard_map/ppermute | solution.py:427
  88.1 12.4 %copy-start.8 = (bf16[128,128]{1,0:T(8,128)(2,1)S(1)}, bf16[128,128]{1,0:T(8,128)(2,1)}, u32[]{:S(2)}) copy-start(bf16[128,128]{1,0:T(8,128)(2,1)} %constant.34.clone.el_ref) | copy-start | bytes 98308
  88.1 12.4 %copy-start.9 = (bf16[128,128]{1,0:T(8,128)(2,1)S(1)}, bf16[128,128]{1,0:T(8,128)(2,1)}, u32[]{:S(2)}) copy-start(bf16[128,128]{1,0:T(8,128)(2,1)} %constant.33.clone.eh_ref) | copy-start | bytes 98308
  88.1 12.4 %copy-start.10 = (f32[8,128]{1,0:T(8,128)S(1)}, f32[8,128]{1,0:T(8,128)}, u32[]{:S(2)}) copy-start(f32[8,128]{1,0:T(8,128)} %get-tuple-element.27.n0_ref) | copy-start | bytes 12292
  88.1 5.3 %collective-permute-start.2 = (f32[128,256]{1,0:T(8,128)S(1)}, f32[128,256]{1,0:T(8,128)S(1)}, u32[]{:S(2)}, u32[]{:S(2)}) collective-permute-start(f32[128,256]{1,0:T(8,128)S(1)} %get-tuple-element.23.own_ref), channel_id=1, source_target_pairs={{0,8},{16,24},{32,40},{48,56},{1,9},{17,25},{33,41},{49,57},{51,59... | collective-permute-start | bytes 393224 | tf_op jit(solution)/shard_map/ppermute | solution.py:428
  88.2 36.5 %copy-start = (bf16[256,512]{1,0:T(8,128)(2,1)S(1)}, bf16[256,512]{1,0:T(8,128)(2,1)}, u32[]{:S(2)}) copy-start(bf16[256,512]{1,0:T(8,128)(2,1)} %constant.27.clone.tl_hbm.tl_ref) | copy-start | bytes 786436
  88.3 36.5 %copy-start.1 = (bf16[256,512]{1,0:T(8,128)(2,1)S(1)}, bf16[256,512]{1,0:T(8,128)(2,1)}, u32[]{:S(2)}) copy-start(bf16[256,512]{1,0:T(8,128)(2,1)} %constant.26.clone.th_hbm.th_ref) | copy-start | bytes 786436
  88.3 36.5 %copy-start.5 = (f32[256,128]{1,0:T(8,128)S(1)}, f32[256,128]{1,0:T(8,128)}, u32[]{:S(2)}) copy-start(f32[256,128]{1,0:T(8,128)} %constant.38.clone.share_ref) | copy-start | bytes 393220
  88.3 5.2 %collective-permute-start.3 = (f32[32,128]{1,0:T(8,128)S(1)}, f32[32,128]{1,0:T(8,128)S(1)}, u32[]{:S(2)}, u32[]{:S(2)}) collective-permute-start(f32[32,128]{1,0:T(8,128)S(1)} %get-tuple-element.24), channel_id=1, source_target_pairs={{0,0},{16,8},{32,24},{48,40},{1,56},{17,9},{33,25},{49,41},{51,57}... | collective-permute-start | bytes 49160 | tf_op jit(solution)/shard_map/ppermute | solution.py:427
  95.3 5.2 %collective-permute-start.4 = (f32[128,256]{1,0:T(8,128)S(1)}, f32[128,256]{1,0:T(8,128)S(1)}, u32[]{:S(2)}, u32[]{:S(2)}) collective-permute-start(f32[128,256]{1,0:T(8,128)S(1)} %get-tuple-element.25.own_ref), channel_id=1, source_target_pairs={{0,8},{16,24},{32,40},{48,56},{1,9},{17,25},{33,41},{49,57},{51,59... | collective-permute-start | bytes 393224 | tf_op jit(solution)/shard_map/ppermute | solution.py:428
  95.4 5.1 %collective-permute-start.5 = (f32[32,128]{1,0:T(8,128)S(1)}, f32[32,128]{1,0:T(8,128)S(1)}, u32[]{:S(2)}, u32[]{:S(2)}) collective-permute-start(f32[32,128]{1,0:T(8,128)S(1)} %get-tuple-element.26), channel_id=1, source_target_pairs={{0,0},{16,8},{32,24},{48,40},{1,56},{17,9},{33,25},{49,41},{51,57}... | collective-permute-start | bytes 49160 | tf_op jit(solution)/shard_map/ppermute | solution.py:427

commit v2 on v1

--- a/solution.py
+++ b/solution.py
@@ -26,6 +26,7 @@
 PACK_LIMIT = 64_200_000
 F32 = jnp.float32
 BF16 = jnp.bfloat16
+SMEM = pl.BlockSpec(memory_space=pltpu.SMEM)
 VMEM = pl.BlockSpec(memory_space=pltpu.VMEM)
 HBM = pl.BlockSpec(memory_space=pltpu.HBM)
 
@@ -50,7 +51,10 @@
 
 PLACES = block_places()
 MIRROR = [(PLACES[o], PLACES[DEV - 1 - o]) for o in range(DEV)]
-MIRROR_EDGE = [(PLACES[o], PLACES[(DEV - o) % DEV]) for o in range(DEV)]
+SELF_EDGE = (0, DEV // 2)
+MIRROR_EDGE = [
+    (PLACES[o], PLACES[DEV // 2 - o if o in SELF_EDGE else DEV - o]) for o in range(DEV)
+]
 
 
 def halves(table):
@@ -201,10 +205,11 @@
     )
 
 
-def mirrored(own_ref, other_ref, edge_ref, flip_tile_ref, flip_cell_ref):
+def mirrored(own_ref, other_ref, sent_ref, edge_ref, alone_ref, flip_tile_ref, flip_cell_ref):
     lane = lax.broadcasted_iota(jnp.int32, (LANES, CELLS), 1)
     other = other_ref[...]
-    edge = jnp.concatenate([unpack_edge(edge_ref[...]), other[:, LANES:]], axis=1)
+    edge = jnp.where(alone_ref[0, 0] > 0, sent_ref[...], edge_ref[...])
+    edge = jnp.concatenate([unpack_edge(edge), other[:, LANES:]], axis=1)
     other = jnp.where(lane < 32, edge, other)
     high, low = split(other)
     flips = flip_tile_ref[...]
@@ -346,18 +351,18 @@
     edge_ref[...] = pack_edge(grid)
 
 
-def next_kernel(own_ref, other_ref, edge_ref, ah_ref, al_ref, mask_ref, ft_ref, fc_ref,
+def next_kernel(own_ref, other_ref, sent_ref, edge_ref, alone_ref, ah_ref, al_ref, mask_ref, ft_ref, fc_ref,
                 out_ref, edge_out_ref, norm_ref):
-    spectrum = mirrored(own_ref, other_ref, edge_ref, ft_ref, fc_ref)
+    spectrum = mirrored(own_ref, other_ref, sent_ref, edge_ref, alone_ref, ft_ref, fc_ref)
     norm_ref[...] = fold(spectrum)
     grid = apply_matrix(spectrum, stored_samples(ah_ref, al_ref), mask_ref)
     out_ref[...] = grid
     edge_out_ref[...] = pack_edge(grid)
 
 
-def send_kernel(own_ref, other_ref, edge_ref, n0_ref, n1_ref, n2_ref, ft_ref, fc_ref,
+def send_kernel(own_ref, other_ref, sent_ref, edge_ref, alone_ref, n0_ref, n1_ref, n2_ref, ft_ref, fc_ref,
                 th_ref, tl_ref, turn_ref, eh_ref, el_ref, out_ref):
-    spectrum = mirrored(own_ref, other_ref, edge_ref, ft_ref, fc_ref)
+    spectrum = mirrored(own_ref, other_ref, sent_ref, edge_ref, alone_ref, ft_ref, fc_ref)
     norms = [jnp.sum(n) for n in (n0_ref[...], n1_ref[...], n2_ref[...], fold(spectrum))]
     data = dot3(load_pair(eh_ref, el_ref), split(swap_chunks(spectrum)))
     re = data[:64].reshape(8, 8, DEV)
@@ -423,10 +428,10 @@
     return out.reshape(rows, LANES)
 
 
-def mirror_exchange(grid, edge):
-    edge = lax.ppermute(edge, AXES, MIRROR_EDGE)
+def mirror_exchange(grid, edge, alone):
+    got = lax.ppermute(edge, AXES, MIRROR_EDGE)
     other = lax.ppermute(grid, AXES, MIRROR)
-    return grid, other, edge
+    return grid, other, edge, got, alone
 
 
 def per_device(image0, interp, vis_weight, counts, tile_index):
@@ -481,22 +486,27 @@
     grid, edge, a_high, a_low, mask = first(
         got, *t["placed"], t["turn"], *t["eight_fwd"], t["spread"]
     )
+    place = lax.axis_index(AXES)
+    alone = (place == PLACES[SELF_EDGE[0]]) | (place == PLACES[SELF_EDGE[1]])
+    alone = alone.astype(jnp.int32).reshape(1, 1)
     norms = [n0]
     follow = call(
         next_kernel,
         [((LANES, CELLS), F32), ((32, LANES), F32), ((8, LANES), F32)],
-        [VMEM] * 8,
+        [VMEM] * 4 + [SMEM] + [VMEM] * 5,
         1_000_000_000,
         3_000_000,
     )
     for _ in range(2):
-        blocks = mirror_exchange(grid, edge)
+        blocks = mirror_exchange(grid, edge, alone)
         grid, edge, norm = follow(
             *blocks, a_high, a_low, mask, t["flip_tile"], t["flip_cell"]
         )
         norms.append(norm)
-    blocks = mirror_exchange(grid, edge)
-    send = call(send_kernel, [((DEV, LANES), F32)], [VMEM] * 13, 300_000_000, 1_500_000)
+    blocks = mirror_exchange(grid, edge, alone)
+    send = call(
+        send_kernel, [((DEV, LANES), F32)], [VMEM] * 4 + [SMEM] + [VMEM] * 10, 300_000_000, 1_500_000
+    )
     (message,) = send(
         *blocks, *norms, t["flip_tile"], t["flip_cell"],
         *t["placed"], t["turn"], *t["eight_inv"],

time: 126 us -> 120 us (0.952)
  starting transfers between devices: 8.79 us -> 3.97 us
  blocking collectives: 97.3 us -> 94.5 us
  waiting for transfers between devices: 6.77 us -> 8.84 us
    ppermute x3, starting transfers between devices: 8.51 us -> 0.74 us  [mirror_exchange(): got = lax.ppermute(edge, AXES, MIRROR_EDGE)]
    ppermute x3, starting transfers between devices: 0.28 us -> 3.23 us  [mirror_exchange(): other = lax.ppermute(grid, AXES, MIRROR)]
    all_to_all x2, blocking collectives: 97.3 us -> 94.5 us  [exchange(): lax.all_to_all(message.reshape(rows, 1, LANES), AXES, 0, 0, tiled=True, a...]
    ppermute x3, waiting for transfers between devices: 6.77 us -> 8.83 us  [mirror_exchange(): got = lax.ppermute(edge, AXES, MIRROR_EDGE)]
where the time goes in v2:
time: 120 us
  blocking collectives  94.5 us (79%)
  Pallas kernels  11.9 us (10%)
  waiting for transfers between devices  8.84 us (7%)
  starting transfers between devices  3.97 us (3%)
    all_to_all x2, blocking collectives, exchange(): lax.all_to_all(message.reshape(rows, 1, LANES), AXES, 0, 0, tiled=True, a...  94.5 us
    ppermute x3, waiting for transfers between devices, mirror_exchange(): got = lax.ppermute(edge, AXES, MIRROR_EDGE)  8.83 us
    pallas_call x1, Pallas kernels, per_device(): pack(image0, interp.reshape(SLOTS, VCAP, CELLS), vis_weight.reshape(SLOTS...  3.81 us
    pallas_call x2, Pallas kernels, per_device(): follow(*blocks, a_high, a_low, mask, t['flip_tile'], t['flip_cell'])  3.71 us
    ppermute x3, starting transfers between devices, mirror_exchange(): other = lax.ppermute(grid, AXES, MIRROR)  3.23 us
  transfers between devices with their start and end apart: 6, of which 3 were waited for; matrix products, arithmetic and copies ran while one was open for 0% of the time, Pallas kernels for 0%

profile of v2, /device:TPU:1, one launch (start us, length us, event | category | flops | bytes accessed | tf_op | source)
XLA Modules:
  0.0 120.1 jit_solution(7643252050437716600)
XLA Ops:
  0.6 3.8 %shard_map.185 = (f32[4608,128]{1,0:T(8,128)}, f32[8,128]{1,0:T(8,128)}) custom-call(f32[8,2048]{1,0:T(8,128)} %image_hbm.1, f32[256,8,256]{2,1,0:T(8,128)} %bitcast.20, f32[8,256]{1,0:T(8,128)} %bitcast.21, s32[1,256]{1,0:T(1,128)} %bitcast.22, s32[1,256]{1,0:T(1,128)} %bitcast.23, bf16[256,512]{1,0:T(8,128)(2,1)} %constant.41.clone.th_hbm.th_ref, ...), custom_call_target="tpu_custom_call" | custom-call | flops 200000000 | bytes 5000000 | tf_op jit(solution)/shard_map/pallas_call | solution.py:463
  4.5 0.0 copy-start.2
  4.5 0.0 copy-start.3
  4.5 0.0 copy-start.4
  4.5 0.0 copy-start.11
  4.5 0.0 copy-start.12
  4.5 0.0 copy-start.13
  4.5 74.3 %all_to_all.10 = f32[4608,1,128]{2,1,0:T(1,128)S(1)} all-to-all(f32[4608,1,128]{2,1,0:T(1,128)} %bitcast.19), channel_id=1, replica_groups={{0,16,32,48,1,17,33,49,51,35,19,3,50,34,18,2,4,20,36,52,5,21,37,53,55,3..., dimensions={0} | all-to-all | bytes 4718592 | tf_op jit(solution)/shard_map/all_to_all | solution.py:425
  78.8 0.0 copy-start.6
  78.8 0.0 copy-start.7
  78.8 0.0 copy-done.2
  78.8 0.0 copy-done.3
  78.9 0.0 copy-done.4
  78.9 0.0 copy-done.11
  78.9 0.0 copy-done.12
  78.9 0.0 copy-done.13
  78.9 2.2 %shard_map.186 = (f32[128,256]{1,0:T(8,128)S(1)}, f32[32,128]{1,0:T(8,128)S(1)}, bf16[2048,256]{1,0:T(8,128)(2,1)S(1)}, bf16[2048,256]{1,0:T(8,128)(2,1)S(1)}, f32[16,256]{1,0:T(8,128)S(1)}) custom-call(f32[4608,128]{1,0:T(8,128)S(1)} %bitcast.16, bf16[256,512]{1,0:T(8,128)(2,1)S(1)} %copy-done.2, bf16[256,512]{1,0:T(8,128)(2,1)S(1)} %copy-done.3, ...), custom_call_target="tpu_custom_call" | custom-call | flops 1000000000 | bytes 5000000 | tf_op jit(solution)/shard_map/pallas_call | solution.py:486
  81.1 0.1 collective-permute-start
  81.2 0.7 collective-permute-start.1
  81.9 2.5 %collective-permute-done.1.edge_ref = f32[32,128]{1,0:T(8,128)S(1)} collective-permute-done((f32[32,128]{1,0:T(8,128)S(1)}, f32[32,128]{1,0:T(8,128)S(1)}, u32[]{:S(2)}, u32[]{:S(2)}) %collective-permute-start.1) | collective-permute-done | bytes 16416 | tf_op jit(solution)/shard_map/ppermute | solution.py:432
  84.4 0.0 collective-permute-done.other_ref
  84.4 0.0 copy-done.6
  84.4 0.0 copy-done.7
  84.4 1.9 %shard_map.187 = (f32[128,256]{1,0:T(8,128)S(1)}, f32[32,128]{1,0:T(8,128)S(1)}, f32[8,128]{1,0:T(8,128)S(1)}) custom-call(f32[128,256]{1,0:T(8,128)S(1)} %get-tuple-element.18.own_ref, f32[128,256]{1,0:T(8,128)S(1)} %collective-permute-done.other_ref, f32[32,128]{1,0:T(8,128)S(1)} %get-tuple-element.19.sent_ref, ...), custom_call_target="tpu_custom_call" | custom-call | flops 1000000000 | bytes 3000000 | tf_op jit(solution)/shard_map/pallas_call | solution.py:502
  86.3 0.0 copy-start.8
  86.3 0.0 copy-start.9
  86.3 0.0 copy-start.10
  86.3 1.7 %collective-permute-start.2 = (f32[128,256]{1,0:T(8,128)S(1)}, f32[128,256]{1,0:T(8,128)S(1)}, u32[]{:S(2)}, u32[]{:S(2)}) collective-permute-start(f32[128,256]{1,0:T(8,128)S(1)} %get-tuple-element.23.own_ref), channel_id=1, source_target_pairs={{0,8},{16,24},{32,40},{48,56},{1,9},{17,25},{33,41},{49,57},{51,59... | collective-permute-start | bytes 393224 | tf_op jit(solution)/shard_map/ppermute | solution.py:433
  88.0 0.0 copy-start
  88.0 0.0 copy-start.1
  88.0 0.0 copy-start.5
  88.0 0.0 collective-permute-start.3
  88.0 3.2 %collective-permute-done.3.edge_ref = f32[32,128]{1,0:T(8,128)S(1)} collective-permute-done((f32[32,128]{1,0:T(8,128)S(1)}, f32[32,128]{1,0:T(8,128)S(1)}, u32[]{:S(2)}, u32[]{:S(2)}) %collective-permute-start.3) | collective-permute-done | bytes 16416 | tf_op jit(solution)/shard_map/ppermute | solution.py:432
  91.2 0.0 collective-permute-done.2.other_ref
  91.2 1.9 %shard_map.188 = (f32[128,256]{1,0:T(8,128)S(1)}, f32[32,128]{1,0:T(8,128)S(1)}, f32[8,128]{1,0:T(8,128)S(1)}) custom-call(f32[128,256]{1,0:T(8,128)S(1)} %get-tuple-element.23.own_ref, f32[128,256]{1,0:T(8,128)S(1)} %collective-permute-done.2.other_ref, f32[32,128]{1,0:T(8,128)S(1)} %get-tuple-element.24.sent_ref, ...), custom_call_target="tpu_custom_call" | custom-call | flops 1000000000 | bytes 3000000 | tf_op jit(solution)/shard_map/pallas_call | solution.py:502
  93.1 1.4 %collective-permute-start.4 = (f32[128,256]{1,0:T(8,128)S(1)}, f32[128,256]{1,0:T(8,128)S(1)}, u32[]{:S(2)}, u32[]{:S(2)}) collective-permute-start(f32[128,256]{1,0:T(8,128)S(1)} %get-tuple-element.25.own_ref), channel_id=1, source_target_pairs={{0,8},{16,24},{32,40},{48,56},{1,9},{17,25},{33,41},{49,57},{51,59... | collective-permute-start | bytes 393224 | tf_op jit(solution)/shard_map/ppermute | solution.py:433
  94.5 0.0 collective-permute-start.5
  94.5 3.2 %collective-permute-done.5.edge_ref = f32[32,128]{1,0:T(8,128)S(1)} collective-permute-done((f32[32,128]{1,0:T(8,128)S(1)}, f32[32,128]{1,0:T(8,128)S(1)}, u32[]{:S(2)}, u32[]{:S(2)}) %collective-permute-start.5) | collective-permute-done | bytes 16416 | tf_op jit(solution)/shard_map/ppermute | solution.py:432
  97.7 0.0 collective-permute-done.4.other_ref
  97.7 0.0 copy-done.8
  97.7 0.0 copy-done.9
  97.7 0.0 copy-done.10
  97.7 1.2 %shard_map.189 = f32[256,128]{1,0:T(8,128)S(1)} custom-call(f32[128,256]{1,0:T(8,128)S(1)} %get-tuple-element.25.own_ref, f32[128,256]{1,0:T(8,128)S(1)} %collective-permute-done.4.other_ref, f32[32,128]{1,0:T(8,128)S(1)} %get-tuple-element.26.sent_ref, f32[32,128]{1,0:T(8,128)S(1)} %collective-permute-done.5.edge_ref, s32[1,1]{1,0:T(1,128)} %bitcast.8.alone_ref, ...), custom_call_target="tpu_custom_call" | custom-call | flops 300000000 | bytes 1500000 | tf_op jit(solution)/shard_map/pallas_call | solution.py:510
  98.9 20.2 %all_to_all.11 = f32[256,1,128]{2,1,0:T(1,128)S(1)} all-to-all(f32[256,1,128]{2,1,0:T(1,128)S(1)} %bitcast.17), channel_id=1, replica_groups={{0,16,32,48,1,17,33,49,51,35,19,3,50,34,18,2,4,20,36,52,5,21,37,53,55,3..., dimensions={0} | all-to-all | bytes 262144 | tf_op jit(solution)/shard_map/all_to_all | solution.py:425
  119.1 0.0 copy-done
  119.1 0.0 copy-done.1
  119.1 0.0 copy-done.5
  119.2 1.0 shard_map.190
Async XLA Ops:
  4.5 74.4 %copy-start.2 = (bf16[256,512]{1,0:T(8,128)(2,1)S(1)}, bf16[256,512]{1,0:T(8,128)(2,1)}, u32[]{:S(2)}) copy-start(bf16[256,512]{1,0:T(8,128)(2,1)} %constant.43.clone.th_ref) | copy-start | bytes 786436
  4.5 74.4 %copy-start.3 = (bf16[256,512]{1,0:T(8,128)(2,1)S(1)}, bf16[256,512]{1,0:T(8,128)(2,1)}, u32[]{:S(2)}) copy-start(bf16[256,512]{1,0:T(8,128)(2,1)} %constant.44.clone.tl_ref) | copy-start | bytes 786436
  4.5 74.4 %copy-start.4 = (f32[16,256]{1,0:T(8,128)S(1)}, f32[16,256]{1,0:T(8,128)}, u32[]{:S(2)}) copy-start(f32[16,256]{1,0:T(8,128)} %constant.45.clone.turn_hbm.turn_ref) | copy-start | bytes 49156
  4.5 74.4 %copy-start.11 = (bf16[256,256]{1,0:T(8,128)(2,1)S(1)}, bf16[256,256]{1,0:T(8,128)(2,1)}, u32[]{:S(2)}) copy-start(bf16[256,256]{1,0:T(8,128)(2,1)} %constant.52.clone.spread_ref) | copy-start | bytes 393220
  4.5 74.4 %copy-start.12 = (bf16[128,128]{1,0:T(8,128)(2,1)S(1)}, bf16[128,128]{1,0:T(8,128)(2,1)}, u32[]{:S(2)}) copy-start(bf16[128,128]{1,0:T(8,128)(2,1)} %constant.46.clone.eh_ref) | copy-start | bytes 98308
  4.5 74.4 %copy-start.13 = (bf16[128,128]{1,0:T(8,128)(2,1)S(1)}, bf16[128,128]{1,0:T(8,128)(2,1)}, u32[]{:S(2)}) copy-start(bf16[128,128]{1,0:T(8,128)(2,1)} %constant.47.clone.el_ref) | copy-start | bytes 98308
  78.8 5.6 %copy-start.6 = (bf16[256,256]{1,0:T(8,128)(2,1)S(1)}, bf16[256,256]{1,0:T(8,128)(2,1)}, u32[]{:S(2)}) copy-start(bf16[256,256]{1,0:T(8,128)(2,1)} %constant.51.clone.fc_ref) | copy-start | bytes 393220
  78.8 5.6 %copy-start.7 = (bf16[256,128]{1,0:T(8,128)(2,1)S(1)}, bf16[256,128]{1,0:T(8,128)(2,1)}, u32[]{:S(2)}) copy-start(bf16[256,128]{1,0:T(8,128)(2,1)} %constant.50.clone.ft_ref) | copy-start | bytes 196612
  81.1 3.4 %collective-permute-start = (f32[128,256]{1,0:T(8,128)S(1)}, f32[128,256]{1,0:T(8,128)S(1)}, u32[]{:S(2)}, u32[]{:S(2)}) collective-permute-start(f32[128,256]{1,0:T(8,128)S(1)} %get-tuple-element.18.own_ref), channel_id=1, source_target_pairs={{0,8},{16,24},{32,40},{48,56},{1,9},{17,25},{33,41},{49,57},{51,59... | collective-permute-start | bytes 393224 | tf_op jit(solution)/shard_map/ppermute | solution.py:433
  81.2 3.3 %collective-permute-start.1 = (f32[32,128]{1,0:T(8,128)S(1)}, f32[32,128]{1,0:T(8,128)S(1)}, u32[]{:S(2)}, u32[]{:S(2)}) collective-permute-start(f32[32,128]{1,0:T(8,128)S(1)} %get-tuple-element.19.sent_ref), channel_id=1, source_target_pairs={{0,200},{16,8},{32,24},{48,40},{1,56},{17,9},{33,25},{49,41},{51,5... | collective-permute-start | bytes 49160 | tf_op jit(solution)/shard_map/ppermute | solution.py:432
  86.3 11.4 %copy-start.8 = (bf16[128,128]{1,0:T(8,128)(2,1)S(1)}, bf16[128,128]{1,0:T(8,128)(2,1)}, u32[]{:S(2)}) copy-start(bf16[128,128]{1,0:T(8,128)(2,1)} %constant.48.clone.eh_ref) | copy-start | bytes 98308
  86.3 11.4 %copy-start.9 = (bf16[128,128]{1,0:T(8,128)(2,1)S(1)}, bf16[128,128]{1,0:T(8,128)(2,1)}, u32[]{:S(2)}) copy-start(bf16[128,128]{1,0:T(8,128)(2,1)} %constant.49.clone.el_ref) | copy-start | bytes 98308
  86.3 11.4 %copy-start.10 = (f32[8,128]{1,0:T(8,128)S(1)}, f32[8,128]{1,0:T(8,128)}, u32[]{:S(2)}) copy-start(f32[8,128]{1,0:T(8,128)} %get-tuple-element.27.n0_ref) | copy-start | bytes 12292
  86.3 4.9 %collective-permute-start.2 = (f32[128,256]{1,0:T(8,128)S(1)}, f32[128,256]{1,0:T(8,128)S(1)}, u32[]{:S(2)}, u32[]{:S(2)}) collective-permute-start(f32[128,256]{1,0:T(8,128)S(1)} %get-tuple-element.23.own_ref), channel_id=1, source_target_pairs={{0,8},{16,24},{32,40},{48,56},{1,9},{17,25},{33,41},{49,57},{51,59... | collective-permute-start | bytes 393224 | tf_op jit(solution)/shard_map/ppermute | solution.py:433
  88.0 31.1 %copy-start = (bf16[256,512]{1,0:T(8,128)(2,1)S(1)}, bf16[256,512]{1,0:T(8,128)(2,1)}, u32[]{:S(2)}) copy-start(bf16[256,512]{1,0:T(8,128)(2,1)} %constant.41.clone.th_hbm.th_ref) | copy-start | bytes 786436
  88.0 31.1 %copy-start.1 = (bf16[256,512]{1,0:T(8,128)(2,1)S(1)}, bf16[256,512]{1,0:T(8,128)(2,1)}, u32[]{:S(2)}) copy-start(bf16[256,512]{1,0:T(8,128)(2,1)} %constant.42.clone.tl_hbm.tl_ref) | copy-start | bytes 786436
  88.0 31.1 %copy-start.5 = (f32[256,128]{1,0:T(8,128)S(1)}, f32[256,128]{1,0:T(8,128)}, u32[]{:S(2)}) copy-start(f32[256,128]{1,0:T(8,128)} %constant.53.clone.share_ref) | copy-start | bytes 393220
  88.0 3.2 %collective-permute-start.3 = (f32[32,128]{1,0:T(8,128)S(1)}, f32[32,128]{1,0:T(8,128)S(1)}, u32[]{:S(2)}, u32[]{:S(2)}) collective-permute-start(f32[32,128]{1,0:T(8,128)S(1)} %get-tuple-element.24.sent_ref), channel_id=1, source_target_pairs={{0,200},{16,8},{32,24},{48,40},{1,56},{17,9},{33,25},{49,41},{51,5... | collective-permute-start | bytes 49160 | tf_op jit(solution)/shard_map/ppermute | solution.py:432
  93.1 4.6 %collective-permute-start.4 = (f32[128,256]{1,0:T(8,128)S(1)}, f32[128,256]{1,0:T(8,128)S(1)}, u32[]{:S(2)}, u32[]{:S(2)}) collective-permute-start(f32[128,256]{1,0:T(8,128)S(1)} %get-tuple-element.25.own_ref), channel_id=1, source_target_pairs={{0,8},{16,24},{32,40},{48,56},{1,9},{17,25},{33,41},{49,57},{51,59... | collective-permute-start | bytes 393224 | tf_op jit(solution)/shard_map/ppermute | solution.py:433
  94.5 3.2 %collective-permute-start.5 = (f32[32,128]{1,0:T(8,128)S(1)}, f32[32,128]{1,0:T(8,128)S(1)}, u32[]{:S(2)}, u32[]{:S(2)}) collective-permute-start(f32[32,128]{1,0:T(8,128)S(1)} %get-tuple-element.26.sent_ref), channel_id=1, source_target_pairs={{0,200},{16,8},{32,24},{48,40},{1,56},{17,9},{33,25},{49,41},{51,5... | collective-permute-start | bytes 49160 | tf_op jit(solution)/shard_map/ppermute | solution.py:432

commit v3 on v2

--- a/solution.py
+++ b/solution.py
@@ -33,10 +33,12 @@
 
 def chip_path():
     path = []
-    for x in range(4):
-        for step_y, y in enumerate(range(4) if x % 2 == 0 else range(3, -1, -1)):
-            zs = range(8) if (x * 4 + step_y) % 2 == 0 else range(7, -1, -1)
-            path.extend((x, y, z) for z in zs)
+    for z in range(8):
+        plane = []
+        for y in range(4):
+            xs = range(4) if y % 2 == 0 else range(3, -1, -1)
+            plane.extend((x, y, z) for x in xs)
+        path.extend(plane if z % 2 == 0 else plane[::-1])
     return path
 
 
@@ -75,9 +77,13 @@
     for name, rows in (("plain", index), ("placed", np.array(PLACES))):
         cos, sin = turns(rows[:, None] * index[None, :], DEV)
         out[name] = halves(np.concatenate([cos, sin], axis=1))
+    few = np.arange(16)
+    coarse = turns(few[:, None] * index[None, :], 16)
+    fine = turns(few[:, None] * index[None, :], DEV)
     small = np.arange(8)
     cos, sin = turns(small[:, None] * index[None, :], N)
     out["turn"] = np.concatenate([cos, sin], axis=0).astype(np.float32)
+    out["start"] = np.concatenate([cos, sin, *fine, *coarse], axis=0).astype(np.float32)
     cos8, sin8 = turns(small[:, None] * small[None, :], 8)
     eye = np.eye(8)
     cos, sin = np.kron(eye, cos8), np.kron(eye, sin8)
@@ -221,13 +227,13 @@
     return 0.5 * (own_ref[...] + (turned[:LANES] + turned[LANES:]))
 
 
-def pack_kernel(image_hbm, interp_hbm, weight_hbm, index_hbm, counts_hbm, th_hbm, tl_hbm, turn_hbm,
-                out_hbm, norm_ref, out_ref, image_ref, held, weight_ref, index_ref, counts_ref,
-                th_ref, tl_ref, turn_ref, sems):
+def pack_kernel(image_hbm, interp_hbm, weight_hbm, index_hbm, counts_hbm, turn_hbm,
+                out_hbm, out_ref, image_ref, held, weight_ref, index_ref, counts_ref,
+                turn_ref, table_ref, sems):
     pieces = 8
     size = SLOTS // pieces
     pairs = [
-        (image_hbm, image_ref), (turn_hbm, turn_ref), (th_hbm, th_ref), (tl_hbm, tl_ref),
+        (turn_hbm, turn_ref), (image_hbm, image_ref),
         (index_hbm, index_ref), (counts_hbm, counts_ref), (weight_hbm, weight_ref),
     ]
     pairs += [
@@ -241,14 +247,15 @@
     for copy in copies:
         copy.start()
     copies[0].wait()
+    cos_b, sin_b = turn_ref[16:32, :], turn_ref[32:48, :]
+    for a in range(16):
+        cos_a, sin_a = turn_ref[48 + a : 49 + a, :], turn_ref[64 + a : 65 + a, :]
+        rows = slice(a * 16, a * 16 + 16)
+        table_ref[0, rows, :DEV], table_ref[1, rows, :DEV] = split(cos_a * cos_b - sin_a * sin_b)
+        table_ref[0, rows, DEV:], table_ref[1, rows, DEV:] = split(sin_a * cos_b + cos_a * sin_b)
     copies[1].wait()
     image = image_ref[...]
     x = [image[:, q * 256 : (q + 1) * 256] for q in range(8)]
-    squares = None
-    for q in range(8):
-        both = x[q][:, :LANES] ** 2 + x[q][:, LANES:] ** 2
-        squares = both if squares is None else squares + both
-    norm_ref[...] = squares
     re, im = [None] * 8, [None] * 8
     for c in range(5):
         cos = [math.cos(2.0 * math.pi * (c * q % 8) / 8) for q in range(8)]
@@ -266,11 +273,9 @@
     plain = jnp.concatenate(turned_re + turned_im, axis=0)
     crossed = jnp.concatenate(turned_im + [-v for v in turned_re], axis=0)
     data = split(jnp.concatenate([plain, crossed], axis=1))
-    copies[2].wait()
-    copies[3].wait()
-    columns = dot3(load_pair(th_ref, tl_ref), data, NT)
+    columns = dot3((table_ref[0], table_ref[1]), data, NT)
     out_ref[pl.ds(16, DEV, stride=MSG), :] = columns
-    for i in (4, 5, 6):
+    for i in (2, 3, 4):
         copies[i].wait()
     marks = jnp.concatenate(
         [
@@ -296,11 +301,11 @@
     rows = size * MSG
     sent = []
     for i in range(pieces):
-        copies[7 + i].wait()
+        copies[5 + i].wait()
         lax.fori_loop(i * groups, (i + 1) * groups, move, 0, unroll=2)
         part = pl.ds(i * rows, rows)
         sent.append(
-            pltpu.make_async_copy(out_ref.at[part], out_hbm.at[part], sems.at[15 + i])
+            pltpu.make_async_copy(out_ref.at[part], out_hbm.at[part], sems.at[13 + i])
         )
         sent[-1].start()
     for copy in sent:
@@ -308,7 +313,7 @@
 
 
 def first_kernel(got_ref, th_ref, tl_ref, turn_ref, eh_ref, el_ref, spread_ref,
-                 out_ref, edge_ref, ah_ref, al_ref, mask_ref):
+                 out_ref, edge_ref, ah_ref, al_ref, mask_ref, norm_ref):
     def samples(m):
         slots = [
             jnp.concatenate(
@@ -346,7 +351,9 @@
     cos, sin = turn_ref[:8, :] * scale, turn_ref[8:, :] * scale
     turned = jnp.concatenate([re * cos + im * sin, im * cos - re * sin], axis=0)
     spectrum = dot3(load_pair(eh_ref, el_ref), split(turned.reshape(LANES, DEV)))
-    grid = apply_matrix(swap_chunks(spectrum), samples, mask_ref)
+    spectrum = swap_chunks(spectrum)
+    norm_ref[...] = fold(spectrum)
+    grid = apply_matrix(spectrum, samples, mask_ref)
     out_ref[...] = grid
     edge_ref[...] = pack_edge(grid)
 
@@ -384,7 +391,7 @@
     got = got_ref[...]
     totals = jnp.sum(got, axis=0, keepdims=True)
     norms = [jnp.sqrt(totals[:, NORM_LANE + i : NORM_LANE + i + 1]) for i in range(4)]
-    first = norms[1] / (norms[0] * START_SCALE)
+    first = norms[1] / norms[0]
     rest = [norms[2] / norms[1], norms[3] / norms[2]]
     lane = lax.broadcasted_iota(jnp.int32, (1, 3), 1)
     found_ref[...] = jnp.where(lane == 0, first, jnp.where(lane == 1, rest[0], rest[1]))
@@ -441,8 +448,8 @@
     }
     pack = call(
         pack_kernel,
-        [((DEV * MSG, LANES), F32), ((8, LANES), F32)],
-        [HBM] * 8,
+        [((DEV * MSG, LANES), F32)],
+        [HBM] * 6,
         200_000_000,
         5_000_000,
         scratch=[
@@ -452,22 +459,20 @@
             pltpu.VMEM((VCAP, SLOTS), F32),
             pltpu.VMEM((1, SLOTS), jnp.int32),
             pltpu.VMEM((1, SLOTS), jnp.int32),
-            pltpu.VMEM((DEV, 2 * DEV), BF16),
-            pltpu.VMEM((DEV, 2 * DEV), BF16),
-            pltpu.VMEM((16, DEV), F32),
-            pltpu.SemaphoreType.DMA((23,)),
+            pltpu.VMEM((80, DEV), F32),
+            pltpu.VMEM((2, DEV, 2 * DEV), BF16),
+            pltpu.SemaphoreType.DMA((21,)),
         ],
         limit=PACK_LIMIT,
-        out_specs=(HBM, VMEM),
-    )
-    message, n0 = pack(
+        out_specs=(HBM,),
+    )
+    (message,) = pack(
         image0,
         interp.reshape(SLOTS, VCAP, CELLS),
         vis_weight.reshape(SLOTS, VCAP).T,
         tile_index.reshape(1, SLOTS),
         counts.reshape(1, SLOTS),
-        *t["plain"],
-        t["turn"],
+        t["start"],
     )
     got = exchange(message)
     first = call(
@@ -478,12 +483,13 @@
             ((SAMPLES, CELLS), BF16),
             ((SAMPLES, CELLS), BF16),
             ((16, 256), F32),
+            ((8, LANES), F32),
         ],
         [VMEM] * 7,
         1_000_000_000,
         5_000_000,
     )
-    grid, edge, a_high, a_low, mask = first(
+    grid, edge, a_high, a_low, mask, n0 = first(
         got, *t["placed"], t["turn"], *t["eight_fwd"], t["spread"]
     )
     place = lax.axis_index(AXES)

time: 120 us -> 119 us (level)
  no operation moved by 1% of the time
where the time goes in v3:
time: 119 us; the launch traced here: 118 us
  blocking collectives  93.5 us (79%)
  Pallas kernels  11.3 us (9%)
  waiting for transfers between devices  8.3 us (7%)
  starting transfers between devices  4.51 us (4%)
    all_to_all x2, blocking collectives, exchange(): lax.all_to_all(message.reshape(rows, 1, LANES), AXES, 0, 0, tiled=True, a...  93.5 us
    ppermute x3, waiting for transfers between devices, mirror_exchange(): got = lax.ppermute(edge, AXES, MIRROR_EDGE)  8.29 us
    pallas_call x2, Pallas kernels, per_device(): follow(*blocks, a_high, a_low, mask, t['flip_tile'], t['flip_cell'])  3.74 us
    ppermute x3, starting transfers between devices, mirror_exchange(): other = lax.ppermute(grid, AXES, MIRROR)  3.23 us
    pallas_call x1, Pallas kernels, per_device(): pack(image0, interp.reshape(SLOTS, VCAP, CELLS), vis_weight.reshape(SLOTS...  3.15 us
  transfers between devices with their start and end apart: 6, of which 3 were waited for; matrix products, arithmetic and copies ran while one was open for 0% of the time, Pallas kernels for 0%

profile of v3, /device:TPU:1, one launch (start us, length us, event | category | flops | bytes accessed | tf_op | source)
XLA Modules:
  0.0 118.4 jit_solution(15350594870315218410)
XLA Ops:
  0.6 3.1 %shard_map.194 = f32[4608,128]{1,0:T(8,128)} custom-call(f32[8,2048]{1,0:T(8,128)} %image_hbm.1, f32[256,8,256]{2,1,0:T(8,128)} %bitcast.20, f32[8,256]{1,0:T(8,128)} %bitcast.21, s32[1,256]{1,0:T(1,128)} %bitcast.22, s32[1,256]{1,0:T(1,128)} %bitcast.23, f32[80,256]{1,0:T(8,128)} %constant.48.clone.turn_hbm), custom_call_target="tpu_custom_call" | custom-call | flops 200000000 | bytes 5000000 | tf_op jit(solution)/shard_map/pallas_call | solution.py:469
  3.8 0.0 copy-start.2
  3.8 0.0 copy-start.3
  3.8 0.0 copy-start.6
  3.8 0.0 copy-start.10
  3.8 0.0 copy-start.11
  3.8 0.0 copy-start.12
  3.9 74.5 %all_to_all.10 = f32[4608,1,128]{2,1,0:T(1,128)S(1)} all-to-all(f32[4608,1,128]{2,1,0:T(1,128)} %bitcast.19), channel_id=1, replica_groups={{0,64,128,192,194,130,66,2,4,68,132,196,198,134,70,6,22,86,150,214,212,..., dimensions={0} | all-to-all | bytes 4718592 | tf_op jit(solution)/shard_map/all_to_all | solution.py:432
  78.3 0.0 copy-start.5
  78.3 0.0 copy-start.7
  78.3 0.0 copy-done.2
  78.4 0.0 copy-done.3
  78.4 0.0 copy-done.6
  78.4 0.0 copy-done.10
  78.4 0.0 copy-done.11
  78.4 0.0 copy-done.12
  78.4 2.2 %shard_map.195 = (f32[128,256]{1,0:T(8,128)S(1)}, f32[32,128]{1,0:T(8,128)S(1)}, bf16[2048,256]{1,0:T(8,128)(2,1)S(1)}, bf16[2048,256]{1,0:T(8,128)(2,1)S(1)}, f...) custom-call(f32[4608,128]{1,0:T(8,128)S(1)} %bitcast.16, bf16[256,512]{1,0:T(8,128)(2,1)S(1)} %copy-done.2, ...), custom_call_target="tpu_custom_call" | custom-call | flops 1000000000 | bytes 5000000 | tf_op jit(solution)/shard_map/pallas_call | solution.py:492
  80.6 0.1 collective-permute-start
  80.7 1.3 %collective-permute-start.1 = (f32[32,128]{1,0:T(8,128)S(1)}, f32[32,128]{1,0:T(8,128)S(1)}, u32[]{:S(2)}, u32[]{:S(2)}) collective-permute-start(f32[32,128]{1,0:T(8,128)S(1)} %get-tuple-element.17.sent_ref), channel_id=1, source_target_pairs={{0,57},{64,8},{128,72},{192,136},{194,200},{130,202},{66,138},{2,7... | collective-permute-start | bytes 49160 | tf_op jit(solution)/shard_map/ppermute | solution.py:439
  82.0 2.0 %collective-permute-done.1.edge_ref = f32[32,128]{1,0:T(8,128)S(1)} collective-permute-done((f32[32,128]{1,0:T(8,128)S(1)}, f32[32,128]{1,0:T(8,128)S(1)}, u32[]{:S(2)}, u32[]{:S(2)}) %collective-permute-start.1) | collective-permute-done | bytes 16416 | tf_op jit(solution)/shard_map/ppermute | solution.py:439
  83.9 0.0 collective-permute-done.other_ref
  83.9 0.0 copy-done.5
  83.9 0.0 copy-done.7
  83.9 1.9 %shard_map.196 = (f32[128,256]{1,0:T(8,128)S(1)}, f32[32,128]{1,0:T(8,128)S(1)}, f32[8,128]{1,0:T(8,128)S(1)}) custom-call(f32[128,256]{1,0:T(8,128)S(1)} %get-tuple-element.16.own_ref, f32[128,256]{1,0:T(8,128)S(1)} %collective-permute-done.other_ref, f32[32,128]{1,0:T(8,128)S(1)} %get-tuple-element.17.sent_ref, ...), custom_call_target="tpu_custom_call" | custom-call | flops 1000000000 | bytes 3000000 | tf_op jit(solution)/shard_map/pallas_call | solution.py:508
  85.8 0.0 copy-start.8
  85.8 0.0 copy-start.9
  85.8 1.7 %collective-permute-start.2 = (f32[128,256]{1,0:T(8,128)S(1)}, f32[128,256]{1,0:T(8,128)S(1)}, u32[]{:S(2)}, u32[]{:S(2)}) collective-permute-start(f32[128,256]{1,0:T(8,128)S(1)} %get-tuple-element.21.own_ref), channel_id=1, source_target_pairs={{0,8},{64,72},{128,136},{192,200},{194,202},{130,138},{66,74},{2,1... | collective-permute-start | bytes 393224 | tf_op jit(solution)/shard_map/ppermute | solution.py:440
  87.5 0.0 copy-start
  87.5 0.0 copy-start.1
  87.5 0.0 copy-start.4
  87.5 0.0 collective-permute-start.3
  87.6 3.2 %collective-permute-done.3.edge_ref = f32[32,128]{1,0:T(8,128)S(1)} collective-permute-done((f32[32,128]{1,0:T(8,128)S(1)}, f32[32,128]{1,0:T(8,128)S(1)}, u32[]{:S(2)}, u32[]{:S(2)}) %collective-permute-start.3) | collective-permute-done | bytes 16416 | tf_op jit(solution)/shard_map/ppermute | solution.py:439
  90.7 0.0 collective-permute-done.2.other_ref
  90.7 1.9 %shard_map.197 = (f32[128,256]{1,0:T(8,128)S(1)}, f32[32,128]{1,0:T(8,128)S(1)}, f32[8,128]{1,0:T(8,128)S(1)}) custom-call(f32[128,256]{1,0:T(8,128)S(1)} %get-tuple-element.21.own_ref, f32[128,256]{1,0:T(8,128)S(1)} %collective-permute-done.2.other_ref, f32[32,128]{1,0:T(8,128)S(1)} %get-tuple-element.22.sent_ref, ...), custom_call_target="tpu_custom_call" | custom-call | flops 1000000000 | bytes 3000000 | tf_op jit(solution)/shard_map/pallas_call | solution.py:508
  92.6 1.4 %collective-permute-start.4 = (f32[128,256]{1,0:T(8,128)S(1)}, f32[128,256]{1,0:T(8,128)S(1)}, u32[]{:S(2)}, u32[]{:S(2)}) collective-permute-start(f32[128,256]{1,0:T(8,128)S(1)} %get-tuple-element.23.own_ref), channel_id=1, source_target_pairs={{0,8},{64,72},{128,136},{192,200},{194,202},{130,138},{66,74},{2,1... | collective-permute-start | bytes 393224 | tf_op jit(solution)/shard_map/ppermute | solution.py:440
  94.0 0.0 collective-permute-start.5
  94.0 3.2 %collective-permute-done.5.edge_ref = f32[32,128]{1,0:T(8,128)S(1)} collective-permute-done((f32[32,128]{1,0:T(8,128)S(1)}, f32[32,128]{1,0:T(8,128)S(1)}, u32[]{:S(2)}, u32[]{:S(2)}) %collective-permute-start.5) | collective-permute-done | bytes 16416 | tf_op jit(solution)/shard_map/ppermute | solution.py:439
  97.2 0.0 collective-permute-done.4.other_ref
  97.2 0.0 copy-done.8
  97.2 0.0 copy-done.9
  97.2 1.2 %shard_map.198 = f32[256,128]{1,0:T(8,128)S(1)} custom-call(f32[128,256]{1,0:T(8,128)S(1)} %get-tuple-element.23.own_ref, f32[128,256]{1,0:T(8,128)S(1)} %collective-permute-done.4.other_ref, f32[32,128]{1,0:T(8,128)S(1)} %get-tuple-element.24.sent_ref, f32[32,128]{1,0:T(8,128)S(1)} %collective-permute-done.5.edge_ref, s32[1,1]{1,0:T(1,128)} %bitcast.8.alone_ref, ...), custom_call_target="tpu_custom_call" | custom-call | flops 300000000 | bytes 1500000 | tf_op jit(solution)/shard_map/pallas_call | solution.py:516
  98.4 19.0 %all_to_all.11 = f32[256,1,128]{2,1,0:T(1,128)S(1)} all-to-all(f32[256,1,128]{2,1,0:T(1,128)S(1)} %bitcast.17), channel_id=1, replica_groups={{0,64,128,192,194,130,66,2,4,68,132,196,198,134,70,6,22,86,150,214,212,..., dimensions={0} | all-to-all | bytes 262144 | tf_op jit(solution)/shard_map/all_to_all | solution.py:432
  117.4 0.0 copy-done
  117.4 0.0 copy-done.1
  117.4 0.0 copy-done.4
  117.4 1.0 shard_map.199
Async XLA Ops:
  3.8 74.6 %copy-start.2 = (bf16[256,512]{1,0:T(8,128)(2,1)S(1)}, bf16[256,512]{1,0:T(8,128)(2,1)}, u32[]{:S(2)}) copy-start(bf16[256,512]{1,0:T(8,128)(2,1)} %constant.45.clone.th_ref) | copy-start | bytes 786436
  3.8 74.6 %copy-start.3 = (bf16[256,512]{1,0:T(8,128)(2,1)S(1)}, bf16[256,512]{1,0:T(8,128)(2,1)}, u32[]{:S(2)}) copy-start(bf16[256,512]{1,0:T(8,128)(2,1)} %constant.46.clone.tl_ref) | copy-start | bytes 786436
  3.8 74.5 %copy-start.6 = (f32[16,256]{1,0:T(8,128)S(1)}, f32[16,256]{1,0:T(8,128)}, u32[]{:S(2)}) copy-start(f32[16,256]{1,0:T(8,128)} %constant.47.clone.turn_ref) | copy-start | bytes 49156
  3.8 74.5 %copy-start.10 = (bf16[256,256]{1,0:T(8,128)(2,1)S(1)}, bf16[256,256]{1,0:T(8,128)(2,1)}, u32[]{:S(2)}) copy-start(bf16[256,256]{1,0:T(8,128)(2,1)} %constant.55.clone.spread_ref) | copy-start | bytes 393220
  3.8 74.5 %copy-start.11 = (bf16[128,128]{1,0:T(8,128)(2,1)S(1)}, bf16[128,128]{1,0:T(8,128)(2,1)}, u32[]{:S(2)}) copy-start(bf16[128,128]{1,0:T(8,128)(2,1)} %constant.49.clone.eh_ref) | copy-start | bytes 98308
  3.8 74.5 %copy-start.12 = (bf16[128,128]{1,0:T(8,128)(2,1)S(1)}, bf16[128,128]{1,0:T(8,128)(2,1)}, u32[]{:S(2)}) copy-start(bf16[128,128]{1,0:T(8,128)(2,1)} %constant.50.clone.el_ref) | copy-start | bytes 98308
  78.3 5.6 %copy-start.5 = (bf16[256,256]{1,0:T(8,128)(2,1)S(1)}, bf16[256,256]{1,0:T(8,128)(2,1)}, u32[]{:S(2)}) copy-start(bf16[256,256]{1,0:T(8,128)(2,1)} %constant.54.clone.fc_ref) | copy-start | bytes 393220
  78.3 5.6 %copy-start.7 = (bf16[256,128]{1,0:T(8,128)(2,1)S(1)}, bf16[256,128]{1,0:T(8,128)(2,1)}, u32[]{:S(2)}) copy-start(bf16[256,128]{1,0:T(8,128)(2,1)} %constant.53.clone.ft_ref) | copy-start | bytes 196612
  80.6 3.4 %collective-permute-start = (f32[128,256]{1,0:T(8,128)S(1)}, f32[128,256]{1,0:T(8,128)S(1)}, u32[]{:S(2)}, u32[]{:S(2)}) collective-permute-start(f32[128,256]{1,0:T(8,128)S(1)} %get-tuple-element.16.own_ref), channel_id=1, source_target_pairs={{0,8},{64,72},{128,136},{192,200},{194,202},{130,138},{66,74},{2,1... | collective-permute-start | bytes 393224 | tf_op jit(solution)/shard_map/ppermute | solution.py:440
  80.7 3.3 %collective-permute-start.1 = (f32[32,128]{1,0:T(8,128)S(1)}, f32[32,128]{1,0:T(8,128)S(1)}, u32[]{:S(2)}, u32[]{:S(2)}) collective-permute-start(f32[32,128]{1,0:T(8,128)S(1)} %get-tuple-element.17.sent_ref), channel_id=1, source_target_pairs={{0,57},{64,8},{128,72},{192,136},{194,200},{130,202},{66,138},{2,7... | collective-permute-start | bytes 49160 | tf_op jit(solution)/shard_map/ppermute | solution.py:439
  85.8 11.4 %copy-start.8 = (bf16[128,128]{1,0:T(8,128)(2,1)S(1)}, bf16[128,128]{1,0:T(8,128)(2,1)}, u32[]{:S(2)}) copy-start(bf16[128,128]{1,0:T(8,128)(2,1)} %constant.51.clone.eh_ref) | copy-start | bytes 98308
  85.8 11.4 %copy-start.9 = (bf16[128,128]{1,0:T(8,128)(2,1)S(1)}, bf16[128,128]{1,0:T(8,128)(2,1)}, u32[]{:S(2)}) copy-start(bf16[128,128]{1,0:T(8,128)(2,1)} %constant.52.clone.el_ref) | copy-start | bytes 98308
  85.8 4.9 %collective-permute-start.2 = (f32[128,256]{1,0:T(8,128)S(1)}, f32[128,256]{1,0:T(8,128)S(1)}, u32[]{:S(2)}, u32[]{:S(2)}) collective-permute-start(f32[128,256]{1,0:T(8,128)S(1)} %get-tuple-element.21.own_ref), channel_id=1, source_target_pairs={{0,8},{64,72},{128,136},{192,200},{194,202},{130,138},{66,74},{2,1... | collective-permute-start | bytes 393224 | tf_op jit(solution)/shard_map/ppermute | solution.py:440
  87.5 29.9 %copy-start = (bf16[256,512]{1,0:T(8,128)(2,1)S(1)}, bf16[256,512]{1,0:T(8,128)(2,1)}, u32[]{:S(2)}) copy-start(bf16[256,512]{1,0:T(8,128)(2,1)} %constant.43.clone.th_ref) | copy-start | bytes 786436
  87.5 29.9 %copy-start.1 = (bf16[256,512]{1,0:T(8,128)(2,1)S(1)}, bf16[256,512]{1,0:T(8,128)(2,1)}, u32[]{:S(2)}) copy-start(bf16[256,512]{1,0:T(8,128)(2,1)} %constant.44.clone.tl_ref) | copy-start | bytes 786436
  87.5 29.9 %copy-start.4 = (f32[256,128]{1,0:T(8,128)S(1)}, f32[256,128]{1,0:T(8,128)}, u32[]{:S(2)}) copy-start(f32[256,128]{1,0:T(8,128)} %constant.56.clone.share_ref) | copy-start | bytes 393220
  87.5 3.2 %collective-permute-start.3 = (f32[32,128]{1,0:T(8,128)S(1)}, f32[32,128]{1,0:T(8,128)S(1)}, u32[]{:S(2)}, u32[]{:S(2)}) collective-permute-start(f32[32,128]{1,0:T(8,128)S(1)} %get-tuple-element.22.sent_ref), channel_id=1, source_target_pairs={{0,57},{64,8},{128,72},{192,136},{194,200},{130,202},{66,138},{2,7... | collective-permute-start | bytes 49160 | tf_op jit(solution)/shard_map/ppermute | solution.py:439
  92.6 4.6 %collective-permute-start.4 = (f32[128,256]{1,0:T(8,128)S(1)}, f32[128,256]{1,0:T(8,128)S(1)}, u32[]{:S(2)}, u32[]{:S(2)}) collective-permute-start(f32[128,256]{1,0:T(8,128)S(1)} %get-tuple-element.23.own_ref), channel_id=1, source_target_pairs={{0,8},{64,72},{128,136},{192,200},{194,202},{130,138},{66,74},{2,1... | collective-permute-start | bytes 393224 | tf_op jit(solution)/shard_map/ppermute | solution.py:440
  94.0 3.2 %collective-permute-start.5 = (f32[32,128]{1,0:T(8,128)S(1)}, f32[32,128]{1,0:T(8,128)S(1)}, u32[]{:S(2)}, u32[]{:S(2)}) collective-permute-start(f32[32,128]{1,0:T(8,128)S(1)} %get-tuple-element.24.sent_ref), channel_id=1, source_target_pairs={{0,57},{64,8},{128,72},{192,136},{194,200},{130,202},{66,138},{2,7... | collective-permute-start | bytes 49160 | tf_op jit(solution)/shard_map/ppermute | solution.py:439

commit v4 on v3

--- a/solution.py
+++ b/solution.py
@@ -19,8 +19,9 @@
 VCAP = 8
 SAMPLES = SLOTS * VCAP
 LANES = 128
-MSG = 18
-GROUP = 4
+MSG = 17
+MARK_LANE = 40
+GROUP = 8
 START_SCALE = 2.0**-11
 NORM_LANE = 40
 PACK_LIMIT = 64_200_000
@@ -103,8 +104,6 @@
     flip = np.zeros((CELLS, CELLS))
     flip[target, cell] = 1.0
     out["flip_cell"] = flip.astype(ml_dtypes.bfloat16)
-    spread = (index[:, None] % 32 == index[None, :] // 8).astype(ml_dtypes.bfloat16)
-    out["spread"] = spread
     share = np.zeros((DEV, 8))
     share[: DEV // 2, :4] = 2.0
     share[DEV // 2 :, 1:5] = 2.0
@@ -274,19 +273,21 @@
     crossed = jnp.concatenate(turned_im + [-v for v in turned_re], axis=0)
     data = split(jnp.concatenate([plain, crossed], axis=1))
     columns = dot3((table_ref[0], table_ref[1]), data, NT)
-    out_ref[pl.ds(16, DEV, stride=MSG), :] = columns
     for i in (2, 3, 4):
         copies[i].wait()
     marks = jnp.concatenate(
         [
+            jnp.zeros((MARK_LANE, SLOTS), F32),
             weight_ref[...],
             index_ref[...].astype(F32),
             counts_ref[...].astype(F32),
-            jnp.zeros((LANES - 10, SLOTS), F32),
+            jnp.zeros((LANES - MARK_LANE - 10, SLOTS), F32),
         ],
         axis=0,
     )
-    out_ref[pl.ds(17, DEV, stride=MSG), :] = marks.T
+    lane = lax.broadcasted_iota(jnp.int32, (DEV, LANES), 1)
+    here = (lane >= MARK_LANE) & (lane < 64)
+    out_ref[pl.ds(16, DEV, stride=MSG), :] = jnp.where(here, marks.T, columns)
 
     def move(group, carry):
         base = pl.multiple_of(group * (GROUP * MSG), 8)
@@ -312,26 +313,32 @@
         copy.wait()
 
 
-def first_kernel(got_ref, th_ref, tl_ref, turn_ref, eh_ref, el_ref, spread_ref,
-                 out_ref, edge_ref, ah_ref, al_ref, mask_ref, norm_ref):
-    def samples(m):
-        slots = [
+def row_kernel(got_ref, row_ref):
+    row_ref[...] = got_ref[pl.ds(16, DEV, stride=MSG), :]
+
+
+def unpack_kernel(got_ref, row_ref, ah_ref, al_ref, mask_ref, turned_ref):
+    for pair in range(SLOTS // 2):
+        rows = [
             jnp.concatenate(
                 [got_ref[pl.ds(slot * MSG + t * 8, 8), :] for t in range(2)], axis=1
             )
-            for slot in range(m * 32, m * 32 + 32)
+            for slot in (2 * pair, 2 * pair + 1)
         ]
-        high, low = split(jnp.concatenate(slots, axis=0))
-        ah_ref[pl.ds(m * 256, 256), :] = high
-        al_ref[pl.ds(m * 256, 256), :] = low
-        return high, low
-
-    marks = got_ref[pl.ds(17, DEV, stride=MSG), :].T[:16]
+        high, low = split(jnp.concatenate(rows, axis=0))
+        ah_ref[pl.ds(pair * 16, 16), :] = high
+        al_ref[pl.ds(pair * 16, 16), :] = low
+
+    turned = row_ref[...].T
+    turned_ref[...] = turned
+    marks = turned[MARK_LANE : MARK_LANE + 16]
     chunk = lax.broadcasted_iota(jnp.int32, (16, SLOTS), 1) // 32
     stacked = jnp.concatenate([jnp.where(chunk == m, marks, 0.0) for m in range(8)], axis=0)
     high, low = split(stacked)
     lowest = (stacked - high.astype(F32) - low.astype(F32)).astype(BF16)
-    spread = spread_ref[...]
+    slot = lax.broadcasted_iota(jnp.int32, (SLOTS, 256), 0) % 32
+    spread = slot == lax.broadcasted_iota(jnp.int32, (SLOTS, 256), 1) // VCAP
+    spread = jnp.where(spread, 1.0, 0.0).astype(BF16)
     spread_marks = dot(high, spread) + (dot(low, spread) + dot(lowest, spread))
     sample = lax.broadcasted_iota(jnp.int32, (8, 256), 1) % 8
     row = lax.broadcasted_iota(jnp.int32, (8, 256), 0)
@@ -342,7 +349,15 @@
         mask_ref[m : m + 1, :] = jnp.where(live, weight, 0.0)
         mask_ref[8 + m : 9 + m, :] = block[8:9]
 
-    columns = got_ref[pl.ds(16, DEV, stride=MSG), :].T
+
+def first_kernel(turned_ref, other_ref, ah_ref, al_ref, mask_ref, th_ref, tl_ref, turn_ref,
+                 eh_ref, el_ref, out_ref, edge_ref, norm_ref):
+    own, other = turned_ref[...], other_ref[...].T
+    columns = jnp.concatenate(
+        [own[:40]] + [other[c * 8 : c * 8 + 8] for c in (3, 2, 1)]
+        + [own[64:104]] + [-other[64 + c * 8 : 72 + c * 8] for c in (3, 2, 1)],
+        axis=0,
+    )
     both = dot3(split(columns), load_pair(th_ref, tl_ref))
     by_cos, by_sin = both[:, :DEV], both[:, DEV:]
     re = (by_cos[:64] + by_sin[64:]).reshape(8, 8, DEV)
@@ -353,7 +368,7 @@
     spectrum = dot3(load_pair(eh_ref, el_ref), split(turned.reshape(LANES, DEV)))
     spectrum = swap_chunks(spectrum)
     norm_ref[...] = fold(spectrum)
-    grid = apply_matrix(spectrum, samples, mask_ref)
+    grid = apply_matrix(spectrum, stored_samples(ah_ref, al_ref), mask_ref)
     out_ref[...] = grid
     edge_ref[...] = pack_edge(grid)
 
@@ -475,22 +490,24 @@
         t["start"],
     )
     got = exchange(message)
+    (row,) = call(row_kernel, [((DEV, LANES), F32)], [VMEM], 100_000, 300_000)(got)
+    other = lax.ppermute(row, AXES, MIRROR)
+    a_high, a_low, mask, turned = call(
+        unpack_kernel,
+        [((SAMPLES, CELLS), BF16), ((SAMPLES, CELLS), BF16), ((16, 256), F32), ((LANES, DEV), F32)],
+        [VMEM] * 2,
+        100_000_000,
+        5_000_000,
+    )(got, row)
     first = call(
         first_kernel,
-        [
-            ((LANES, CELLS), F32),
-            ((32, LANES), F32),
-            ((SAMPLES, CELLS), BF16),
-            ((SAMPLES, CELLS), BF16),
-            ((16, 256), F32),
-            ((8, LANES), F32),
-        ],
-        [VMEM] * 7,
+        [((LANES, CELLS), F32), ((32, LANES), F32), ((8, LANES), F32)],
+        [VMEM] * 10,
         1_000_000_000,
-        5_000_000,
-    )
-    grid, edge, a_high, a_low, mask, n0 = first(
-        got, *t["placed"], t["turn"], *t["eight_fwd"], t["spread"]
+        3_000_000,
+    )
+    grid, edge, n0 = first(
+        turned, other, a_high, a_low, mask, *t["placed"], t["turn"], *t["eight_fwd"]
     )
     place = lax.axis_index(AXES)
     alone = (place == PLACES[SELF_EDGE[0]]) | (place == PLACES[SELF_EDGE[1]])

time: 119 us -> 117 us (0.983)
  blocking collectives: 93.5 us -> 90.6 us
    all_to_all x2, blocking collectives: 93.5 us -> 90.6 us  [exchange(): lax.all_to_all(message.reshape(rows, 1, LANES), AXES, 0, 0, tiled=True, a...]
    pallas_call x1 -> x3, Pallas kernels: 2.17 us -> 2.87 us  [the longest x1 2.38 us: per_device(): first(turned, other, a_high, a_low, mask, *t['placed'], t['turn'], *t['ei...]
  transfers between devices with their start and end apart: 6 -> 7, of which waited for: 3 -> 4; matrix products, arithmetic and copies ran while one was open for 0% -> 0% of each run, Pallas kernels for 0% -> 0%
where the time goes in v4:
time: 117 us
  blocking collectives  90.6 us (77%)
  Pallas kernels  11.9 us (10%)
  waiting for transfers between devices  9.21 us (8%)
  starting transfers between devices  4.52 us (4%)
    all_to_all x2, blocking collectives, exchange(): lax.all_to_all(message.reshape(rows, 1, LANES), AXES, 0, 0, tiled=True, a...  90.6 us
    ppermute x3, waiting for transfers between devices, mirror_exchange(): got = lax.ppermute(edge, AXES, MIRROR_EDGE)  8.37 us
    pallas_call x2, Pallas kernels, per_device(): follow(*blocks, a_high, a_low, mask, t['flip_tile'], t['flip_cell'])  3.73 us
    ppermute x3, starting transfers between devices, mirror_exchange(): other = lax.ppermute(grid, AXES, MIRROR)  3.32 us
    pallas_call x1, Pallas kernels, per_device(): pack(image0, interp.reshape(SLOTS, VCAP, CELLS), vis_weight.reshape(SLOTS...  3.08 us
    pallas_call x1, Pallas kernels, per_device(): first(turned, other, a_high, a_low, mask, *t['placed'], t['turn'], *t['ei...  2.38 us
  transfers between devices with their start and end apart: 7, of which 4 were waited for; matrix products, arithmetic and copies ran while one was open for 0% of the time, Pallas kernels for 0%

profile of v4, /device:TPU:1, one launch (start us, length us, event | category | flops | bytes accessed | tf_op | source)
XLA Modules:
  0.0 117.1 jit_solution(14928611436071791627)
XLA Ops:
  0.6 3.1 %shard_map.185 = f32[4352,128]{1,0:T(8,128)} custom-call(f32[8,2048]{1,0:T(8,128)} %image_hbm.1, f32[256,8,256]{2,1,0:T(8,128)} %bitcast.21, f32[8,256]{1,0:T(8,128)} %bitcast.22, s32[1,256]{1,0:T(1,128)} %bitcast.23, s32[1,256]{1,0:T(1,128)} %bitcast.24, f32[80,256]{1,0:T(8,128)} %constant.46.clone.turn_hbm), custom_call_target="tpu_custom_call" | custom-call | flops 200000000 | bytes 5000000 | tf_op jit(solution)/shard_map/pallas_call | solution.py:484
  3.7 71.7 %all_to_all.10 = f32[4352,1,128]{2,1,0:T(1,128)S(1)} all-to-all(f32[4352,1,128]{2,1,0:T(1,128)} %bitcast.20), channel_id=1, replica_groups={{0,64,128,192,194,130,66,2,4,68,132,196,198,134,70,6,22,86,150,214,212,..., dimensions={0} | all-to-all | bytes 4456448 | tf_op jit(solution)/shard_map/all_to_all | solution.py:447
  75.4 0.0 copy-start.2
  75.4 0.0 copy-start.3
  75.4 0.0 copy-start.6
  75.4 0.0 copy-start.10
  75.4 0.0 copy-start.11
  75.4 0.1 collective-permute-start
  75.5 0.5 shard_map.187
  76.0 0.0 copy-start.5
  76.0 0.0 copy-start.7
  76.0 0.8 collective-permute-done.other_ref
  76.9 0.0 copy-done.2
  76.9 0.0 copy-done.3
  76.9 0.0 copy-done.6
  76.9 0.0 copy-done.10
  76.9 0.0 copy-done.11
  76.9 2.4 %shard_map.188 = (f32[128,256]{1,0:T(8,128)S(1)}, f32[32,128]{1,0:T(8,128)S(1)}, f32[8,128]{1,0:T(8,128)S(1)}) custom-call(f32[128,256]{1,0:T(8,128)S(1)} %get-tuple-element.17.turned_ref, f32[256,128]{1,0:T(8,128)S(1)} %collective-permute-done.other_ref, bf16[2048,256]{1,0:T(8,128)(2,1)S(1)} %get-tuple-element.18.ah_ref, ...), custom_call_target="tpu_custom_call" | custom-call | flops 1000000000 | bytes 3000000 | tf_op jit(solution)/shard_map/pallas_call | solution.py:509
  79.3 0.2 collective-permute-start.1
  79.5 1.1 collective-permute-start.2
  80.6 2.1 %collective-permute-done.2.edge_ref = f32[32,128]{1,0:T(8,128)S(1)} collective-permute-done((f32[32,128]{1,0:T(8,128)S(1)}, f32[32,128]{1,0:T(8,128)S(1)}, u32[]{:S(2)}, u32[]{:S(2)}) %collective-permute-start.2) | collective-permute-done | bytes 16416 | tf_op jit(solution)/shard_map/ppermute | solution.py:454
  82.7 0.0 collective-permute-done.1.other_ref
  82.7 0.0 copy-done.5
  82.7 0.0 copy-done.7
  82.7 1.9 %shard_map.189 = (f32[128,256]{1,0:T(8,128)S(1)}, f32[32,128]{1,0:T(8,128)S(1)}, f32[8,128]{1,0:T(8,128)S(1)}) custom-call(f32[128,256]{1,0:T(8,128)S(1)} %get-tuple-element.21.own_ref, f32[128,256]{1,0:T(8,128)S(1)} %collective-permute-done.1.other_ref, f32[32,128]{1,0:T(8,128)S(1)} %get-tuple-element.22.sent_ref, ...), custom_call_target="tpu_custom_call" | custom-call | flops 1000000000 | bytes 3000000 | tf_op jit(solution)/shard_map/pallas_call | solution.py:525
  84.6 0.0 copy-start.8
  84.6 0.0 copy-start.9
  84.6 1.7 %collective-permute-start.3 = (f32[128,256]{1,0:T(8,128)S(1)}, f32[128,256]{1,0:T(8,128)S(1)}, u32[]{:S(2)}, u32[]{:S(2)}) collective-permute-start(f32[128,256]{1,0:T(8,128)S(1)} %get-tuple-element.23.own_ref), channel_id=1, source_target_pairs={{0,8},{64,72},{128,136},{192,200},{194,202},{130,138},{66,74},{2,1... | collective-permute-start | bytes 393224 | tf_op jit(solution)/shard_map/ppermute | solution.py:455
  86.2 0.0 copy-start
  86.2 0.0 copy-start.1
  86.2 0.0 copy-start.4
  86.3 0.0 collective-permute-start.4
  86.3 3.2 %collective-permute-done.4.edge_ref = f32[32,128]{1,0:T(8,128)S(1)} collective-permute-done((f32[32,128]{1,0:T(8,128)S(1)}, f32[32,128]{1,0:T(8,128)S(1)}, u32[]{:S(2)}, u32[]{:S(2)}) %collective-permute-start.4) | collective-permute-done | bytes 16416 | tf_op jit(solution)/shard_map/ppermute | solution.py:454
  89.4 0.0 collective-permute-done.3.other_ref
  89.4 1.9 %shard_map.190 = (f32[128,256]{1,0:T(8,128)S(1)}, f32[32,128]{1,0:T(8,128)S(1)}, f32[8,128]{1,0:T(8,128)S(1)}) custom-call(f32[128,256]{1,0:T(8,128)S(1)} %get-tuple-element.23.own_ref, f32[128,256]{1,0:T(8,128)S(1)} %collective-permute-done.3.other_ref, f32[32,128]{1,0:T(8,128)S(1)} %get-tuple-element.24.sent_ref, ...), custom_call_target="tpu_custom_call" | custom-call | flops 1000000000 | bytes 3000000 | tf_op jit(solution)/shard_map/pallas_call | solution.py:525
  91.3 1.4 %collective-permute-start.5 = (f32[128,256]{1,0:T(8,128)S(1)}, f32[128,256]{1,0:T(8,128)S(1)}, u32[]{:S(2)}, u32[]{:S(2)}) collective-permute-start(f32[128,256]{1,0:T(8,128)S(1)} %get-tuple-element.25.own_ref), channel_id=1, source_target_pairs={{0,8},{64,72},{128,136},{192,200},{194,202},{130,138},{66,74},{2,1... | collective-permute-start | bytes 393224 | tf_op jit(solution)/shard_map/ppermute | solution.py:455
  92.7 0.0 collective-permute-start.6
  92.7 3.2 %collective-permute-done.6.edge_ref = f32[32,128]{1,0:T(8,128)S(1)} collective-permute-done((f32[32,128]{1,0:T(8,128)S(1)}, f32[32,128]{1,0:T(8,128)S(1)}, u32[]{:S(2)}, u32[]{:S(2)}) %collective-permute-start.6) | collective-permute-done | bytes 16416 | tf_op jit(solution)/shard_map/ppermute | solution.py:454
  95.9 0.0 collective-permute-done.5.other_ref
  95.9 0.0 copy-done.8
  95.9 0.0 copy-done.9
  95.9 1.2 %shard_map.191 = f32[256,128]{1,0:T(8,128)S(1)} custom-call(f32[128,256]{1,0:T(8,128)S(1)} %get-tuple-element.25.own_ref, f32[128,256]{1,0:T(8,128)S(1)} %collective-permute-done.5.other_ref, f32[32,128]{1,0:T(8,128)S(1)} %get-tuple-element.26.sent_ref, f32[32,128]{1,0:T(8,128)S(1)} %collective-permute-done.6.edge_ref, s32[1,1]{1,0:T(1,128)} %bitcast.8.alone_ref, ...), custom_call_target="tpu_custom_call" | custom-call | flops 300000000 | bytes 1500000 | tf_op jit(solution)/shard_map/pallas_call | solution.py:533
  97.1 19.0 %all_to_all.11 = f32[256,1,128]{2,1,0:T(1,128)S(1)} all-to-all(f32[256,1,128]{2,1,0:T(1,128)S(1)} %bitcast.18), channel_id=1, replica_groups={{0,64,128,192,194,130,66,2,4,68,132,196,198,134,70,6,22,86,150,214,212,..., dimensions={0} | all-to-all | bytes 262144 | tf_op jit(solution)/shard_map/all_to_all | solution.py:447
  116.1 0.0 copy-done
  116.1 0.0 copy-done.1
  116.1 0.0 copy-done.4
  116.1 1.0 shard_map.192
  (1 shorter events, 0.0 us)
Async XLA Ops:
  75.4 1.5 %copy-start.2 = (bf16[256,512]{1,0:T(8,128)(2,1)S(1)}, bf16[256,512]{1,0:T(8,128)(2,1)}, u32[]{:S(2)}) copy-start(bf16[256,512]{1,0:T(8,128)(2,1)} %constant.43.clone.th_ref) | copy-start | bytes 786436
  75.4 1.5 %copy-start.3 = (bf16[256,512]{1,0:T(8,128)(2,1)S(1)}, bf16[256,512]{1,0:T(8,128)(2,1)}, u32[]{:S(2)}) copy-start(bf16[256,512]{1,0:T(8,128)(2,1)} %constant.44.clone.tl_ref) | copy-start | bytes 786436
  75.4 1.5 %copy-start.6 = (f32[16,256]{1,0:T(8,128)S(1)}, f32[16,256]{1,0:T(8,128)}, u32[]{:S(2)}) copy-start(f32[16,256]{1,0:T(8,128)} %constant.45.clone.turn_ref) | copy-start | bytes 49156
  75.4 1.5 %copy-start.10 = (bf16[128,128]{1,0:T(8,128)(2,1)S(1)}, bf16[128,128]{1,0:T(8,128)(2,1)}, u32[]{:S(2)}) copy-start(bf16[128,128]{1,0:T(8,128)(2,1)} %constant.47.clone.eh_ref) | copy-start | bytes 98308
  75.4 1.5 %copy-start.11 = (bf16[128,128]{1,0:T(8,128)(2,1)S(1)}, bf16[128,128]{1,0:T(8,128)(2,1)}, u32[]{:S(2)}) copy-start(bf16[128,128]{1,0:T(8,128)(2,1)} %constant.48.clone.el_ref) | copy-start | bytes 98308
  75.4 1.4 %collective-permute-start = (f32[256,128]{1,0:T(8,128)S(1)}, f32[256,128]{1,0:T(8,128)S(1)}, u32[]{:S(2)}, u32[]{:S(2)}) collective-permute-start(f32[256,128]{1,0:T(8,128)S(1)} %shard_map.186.row_ref), channel_id=1, source_target_pairs={{0,8},{64,72},{128,136},{192,200},{194,202},{130,138},{66,74},{2,1... | collective-permute-start | bytes 393224 | tf_op jit(solution)/shard_map/ppermute | solution.py:494
  76.0 6.7 %copy-start.5 = (bf16[256,256]{1,0:T(8,128)(2,1)S(1)}, bf16[256,256]{1,0:T(8,128)(2,1)}, u32[]{:S(2)}) copy-start(bf16[256,256]{1,0:T(8,128)(2,1)} %constant.52.clone.fc_ref) | copy-start | bytes 393220
  76.0 6.7 %copy-start.7 = (bf16[256,128]{1,0:T(8,128)(2,1)S(1)}, bf16[256,128]{1,0:T(8,128)(2,1)}, u32[]{:S(2)}) copy-start(bf16[256,128]{1,0:T(8,128)(2,1)} %constant.51.clone.ft_ref) | copy-start | bytes 196612
  79.3 3.4 %collective-permute-start.1 = (f32[128,256]{1,0:T(8,128)S(1)}, f32[128,256]{1,0:T(8,128)S(1)}, u32[]{:S(2)}, u32[]{:S(2)}) collective-permute-start(f32[128,256]{1,0:T(8,128)S(1)} %get-tuple-element.21.own_ref), channel_id=1, source_target_pairs={{0,8},{64,72},{128,136},{192,200},{194,202},{130,138},{66,74},{2,1... | collective-permute-start | bytes 393224 | tf_op jit(solution)/shard_map/ppermute | solution.py:455
  79.5 3.2 %collective-permute-start.2 = (f32[32,128]{1,0:T(8,128)S(1)}, f32[32,128]{1,0:T(8,128)S(1)}, u32[]{:S(2)}, u32[]{:S(2)}) collective-permute-start(f32[32,128]{1,0:T(8,128)S(1)} %get-tuple-element.22.sent_ref), channel_id=1, source_target_pairs={{0,57},{64,8},{128,72},{192,136},{194,200},{130,202},{66,138},{2,7... | collective-permute-start | bytes 49160 | tf_op jit(solution)/shard_map/ppermute | solution.py:454
  84.6 11.3 %copy-start.8 = (bf16[128,128]{1,0:T(8,128)(2,1)S(1)}, bf16[128,128]{1,0:T(8,128)(2,1)}, u32[]{:S(2)}) copy-start(bf16[128,128]{1,0:T(8,128)(2,1)} %constant.49.clone.eh_ref) | copy-start | bytes 98308
  84.6 11.3 %copy-start.9 = (bf16[128,128]{1,0:T(8,128)(2,1)S(1)}, bf16[128,128]{1,0:T(8,128)(2,1)}, u32[]{:S(2)}) copy-start(bf16[128,128]{1,0:T(8,128)(2,1)} %constant.50.clone.el_ref) | copy-start | bytes 98308
  84.6 4.8 %collective-permute-start.3 = (f32[128,256]{1,0:T(8,128)S(1)}, f32[128,256]{1,0:T(8,128)S(1)}, u32[]{:S(2)}, u32[]{:S(2)}) collective-permute-start(f32[128,256]{1,0:T(8,128)S(1)} %get-tuple-element.23.own_ref), channel_id=1, source_target_pairs={{0,8},{64,72},{128,136},{192,200},{194,202},{130,138},{66,74},{2,1... | collective-permute-start | bytes 393224 | tf_op jit(solution)/shard_map/ppermute | solution.py:455
  86.2 29.9 %copy-start = (bf16[256,512]{1,0:T(8,128)(2,1)S(1)}, bf16[256,512]{1,0:T(8,128)(2,1)}, u32[]{:S(2)}) copy-start(bf16[256,512]{1,0:T(8,128)(2,1)} %constant.41.clone.th_ref) | copy-start | bytes 786436
  86.2 29.9 %copy-start.1 = (bf16[256,512]{1,0:T(8,128)(2,1)S(1)}, bf16[256,512]{1,0:T(8,128)(2,1)}, u32[]{:S(2)}) copy-start(bf16[256,512]{1,0:T(8,128)(2,1)} %constant.42.clone.tl_ref) | copy-start | bytes 786436
  86.2 29.9 %copy-start.4 = (f32[256,128]{1,0:T(8,128)S(1)}, f32[256,128]{1,0:T(8,128)}, u32[]{:S(2)}) copy-start(f32[256,128]{1,0:T(8,128)} %constant.53.clone.share_ref) | copy-start | bytes 393220
  86.3 3.2 %collective-permute-start.4 = (f32[32,128]{1,0:T(8,128)S(1)}, f32[32,128]{1,0:T(8,128)S(1)}, u32[]{:S(2)}, u32[]{:S(2)}) collective-permute-start(f32[32,128]{1,0:T(8,128)S(1)} %get-tuple-element.24.sent_ref), channel_id=1, source_target_pairs={{0,57},{64,8},{128,72},{192,136},{194,200},{130,202},{66,138},{2,7... | collective-permute-start | bytes 49160 | tf_op jit(solution)/shard_map/ppermute | solution.py:454
  91.3 4.6 %collective-permute-start.5 = (f32[128,256]{1,0:T(8,128)S(1)}, f32[128,256]{1,0:T(8,128)S(1)}, u32[]{:S(2)}, u32[]{:S(2)}) collective-permute-start(f32[128,256]{1,0:T(8,128)S(1)} %get-tuple-element.25.own_ref), channel_id=1, source_target_pairs={{0,8},{64,72},{128,136},{192,200},{194,202},{130,138},{66,74},{2,1... | collective-permute-start | bytes 393224 | tf_op jit(solution)/shard_map/ppermute | solution.py:455
  92.7 3.2 %collective-permute-start.6 = (f32[32,128]{1,0:T(8,128)S(1)}, f32[32,128]{1,0:T(8,128)S(1)}, u32[]{:S(2)}, u32[]{:S(2)}) collective-permute-start(f32[32,128]{1,0:T(8,128)S(1)} %get-tuple-element.26.sent_ref), channel_id=1, source_target_pairs={{0,57},{64,8},{128,72},{192,136},{194,200},{130,202},{66,138},{2,7... | collective-permute-start | bytes 49160 | tf_op jit(solution)/shard_map/ppermute | solution.py:454

commit v5 on v4

--- a/solution.py
+++ b/solution.py
@@ -175,14 +175,14 @@
     return total
 
 
-def apply_matrix(spectrum, samples, mask_ref):
+def apply_matrix(spectrum, samples, turned_samples, mask_ref):
     parts = split(spectrum)
     row = lax.broadcasted_iota(jnp.int32, (LANES, 256), 0)
     tile = (row % 8 * 8 + row // 8 % 8).astype(F32)
     total = None
     for m in range(SAMPLES // 256):
         a = samples(m)
-        seen = dot3(parts, a, NT)
+        seen = dot3(parts, turned_samples(m))
         weight = mask_ref[m : m + 1, :]
         wanted = mask_ref[8 + m : 9 + m, :]
         kept = jnp.where(tile == wanted, seen * weight, 0.0)
@@ -193,6 +193,10 @@
 
 def stored_samples(ah_ref, al_ref):
     return lambda m: (ah_ref[pl.ds(m * 256, 256), :], al_ref[pl.ds(m * 256, 256), :])
+
+
+def stored_turned(ah_ref, al_ref):
+    return lambda m: (ah_ref[:, pl.ds(m * 256, 256)], al_ref[:, pl.ds(m * 256, 256)])
 
 
 def pack_edge(grid):
@@ -317,17 +321,17 @@
     row_ref[...] = got_ref[pl.ds(16, DEV, stride=MSG), :]
 
 
-def unpack_kernel(got_ref, row_ref, ah_ref, al_ref, mask_ref, turned_ref):
-    for pair in range(SLOTS // 2):
-        rows = [
-            jnp.concatenate(
-                [got_ref[pl.ds(slot * MSG + t * 8, 8), :] for t in range(2)], axis=1
-            )
-            for slot in (2 * pair, 2 * pair + 1)
-        ]
-        high, low = split(jnp.concatenate(rows, axis=0))
-        ah_ref[pl.ds(pair * 16, 16), :] = high
-        al_ref[pl.ds(pair * 16, 16), :] = low
+def unpack_kernel(got_ref, row_ref, ah_ref, al_ref, bh_ref, bl_ref, mask_ref, turned_ref):
+    for part in range(SLOTS // 16):
+        tiles = [[], []]
+        for slot in range(part * 16, part * 16 + 16):
+            for t in range(2):
+                tiles[t].append(got_ref[pl.ds(slot * MSG + t * 8, 8), :])
+        for t in range(2):
+            tile = jnp.concatenate(tiles[t], axis=0)
+            here, there = pl.ds(part * LANES, LANES), pl.ds(t * LANES, LANES)
+            ah_ref[here, there], al_ref[here, there] = split(tile)
+            bh_ref[there, here], bl_ref[there, here] = split(tile.T)
 
     turned = row_ref[...].T
     turned_ref[...] = turned
@@ -350,7 +354,7 @@
         mask_ref[8 + m : 9 + m, :] = block[8:9]
 
 
-def first_kernel(turned_ref, other_ref, ah_ref, al_ref, mask_ref, th_ref, tl_ref, turn_ref,
+def first_kernel(turned_ref, other_ref, ah_ref, al_ref, bh_ref, bl_ref, mask_ref, th_ref, tl_ref, turn_ref,
                  eh_ref, el_ref, out_ref, edge_ref, norm_ref):
     own, other = turned_ref[...], other_ref[...].T
     columns = jnp.concatenate(
@@ -368,16 +372,20 @@
     spectrum = dot3(load_pair(eh_ref, el_ref), split(turned.reshape(LANES, DEV)))
     spectrum = swap_chunks(spectrum)
     norm_ref[...] = fold(spectrum)
-    grid = apply_matrix(spectrum, stored_samples(ah_ref, al_ref), mask_ref)
+    grid = apply_matrix(
+        spectrum, stored_samples(ah_ref, al_ref), stored_turned(bh_ref, bl_ref), mask_ref
+    )
     out_ref[...] = grid
     edge_ref[...] = pack_edge(grid)
 
 
-def next_kernel(own_ref, other_ref, sent_ref, edge_ref, alone_ref, ah_ref, al_ref, mask_ref, ft_ref, fc_ref,
+def next_kernel(own_ref, other_ref, sent_ref, edge_ref, alone_ref, ah_ref, al_ref, bh_ref, bl_ref, mask_ref, ft_ref, fc_ref,
                 out_ref, edge_out_ref, norm_ref):
     spectrum = mirrored(own_ref, other_ref, sent_ref, edge_ref, alone_ref, ft_ref, fc_ref)
     norm_ref[...] = fold(spectrum)
-    grid = apply_matrix(spectrum, stored_samples(ah_ref, al_ref), mask_ref)
+    grid = apply_matrix(
+        spectrum, stored_samples(ah_ref, al_ref), stored_turned(bh_ref, bl_ref), mask_ref
+    )
     out_ref[...] = grid
     edge_out_ref[...] = pack_edge(grid)
 
@@ -492,9 +500,16 @@
     got = exchange(message)
     (row,) = call(row_kernel, [((DEV, LANES), F32)], [VMEM], 100_000, 300_000)(got)
     other = lax.ppermute(row, AXES, MIRROR)
-    a_high, a_low, mask, turned = call(
+    *samples, mask, turned = call(
         unpack_kernel,
-        [((SAMPLES, CELLS), BF16), ((SAMPLES, CELLS), BF16), ((16, 256), F32), ((LANES, DEV), F32)],
+        [
+            ((SAMPLES, CELLS), BF16),
+            ((SAMPLES, CELLS), BF16),
+            ((CELLS, SAMPLES), BF16),
+            ((CELLS, SAMPLES), BF16),
+            ((16, 256), F32),
+            ((LANES, DEV), F32),
+        ],
         [VMEM] * 2,
         100_000_000,
         5_000_000,
@@ -502,12 +517,12 @@
     first = call(
         first_kernel,
         [((LANES, CELLS), F32), ((32, LANES), F32), ((8, LANES), F32)],
-        [VMEM] * 10,
+        [VMEM] * 12,
         1_000_000_000,
         3_000_000,
     )
     grid, edge, n0 = first(
-        turned, other, a_high, a_low, mask, *t["placed"], t["turn"], *t["eight_fwd"]
+        turned, other, *samples, mask, *t["placed"], t["turn"], *t["eight_fwd"]
     )
     place = lax.axis_index(AXES)
     alone = (place == PLACES[SELF_EDGE[0]]) | (place == PLACES[SELF_EDGE[1]])
@@ -516,14 +531,14 @@
     follow = call(
         next_kernel,
         [((LANES, CELLS), F32), ((32, LANES), F32), ((8, LANES), F32)],
-        [VMEM] * 4 + [SMEM] + [VMEM] * 5,
+        [VMEM] * 4 + [SMEM] + [VMEM] * 7,
         1_000_000_000,
         3_000_000,
     )
     for _ in range(2):
         blocks = mirror_exchange(grid, edge, alone)
         grid, edge, norm = follow(
-            *blocks, a_high, a_low, mask, t["flip_tile"], t["flip_cell"]
+            *blocks, *samples, mask, t["flip_tile"], t["flip_cell"]
         )
         norms.append(norm)
     blocks = mirror_exchange(grid, edge, alone)

time: 117 us -> 121 us (1.034)
  local copies, waits for them, and re-layouts: 0.06 us -> 2.73 us
    unnamed x24 -> x38, local copies, waits for them, and re-layouts: 0.06 us -> 2.73 us
  transfers between devices with their start and end apart: 7 -> 7, of which waited for: 4 -> 4; matrix products, arithmetic and copies ran while one was open for 0% -> 0% of each run, Pallas kernels for 0% -> 1%
where the time goes in v5:
time: 121 us
  blocking collectives  90.7 us (75%)
  Pallas kernels  12.9 us (11%)
  waiting for transfers between devices  9.53 us (8%)
  starting transfers between devices  4.16 us (3%)
  local copies, waits for them, and re-layouts  2.73 us (2%)
    all_to_all x2, blocking collectives, exchange(): lax.all_to_all(message.reshape(rows, 1, LANES), AXES, 0, 0, tiled=True, a...  90.7 us
    ppermute x3, waiting for transfers between devices, mirror_exchange(): got = lax.ppermute(edge, AXES, MIRROR_EDGE)  8.98 us
    pallas_call x2, Pallas kernels, per_device(): follow(*blocks, *samples, mask, t['flip_tile'], t['flip_cell'])  4.2 us
    pallas_call x1, Pallas kernels, per_device(): pack(image0, interp.reshape(SLOTS, VCAP, CELLS), vis_weight.reshape(SLOTS...  3.1 us
    ppermute x3, starting transfers between devices, mirror_exchange(): other = lax.ppermute(grid, AXES, MIRROR)  2.86 us
    unnamed x38, local copies, waits for them, and re-layouts  2.73 us
    pallas_call x1, Pallas kernels, per_device(): first(turned, other, *samples, mask, *t['placed'], t['turn'], *t['eight_f...  2.56 us
  transfers between devices with their start and end apart: 7, of which 4 were waited for; matrix products, arithmetic and copies ran while one was open for 0% of the time, Pallas kernels for 1%

profile of v5, /device:TPU:1, one launch (start us, length us, event | category | flops | bytes accessed | tf_op | source)
XLA Modules:
  0.0 120.8 jit_solution(11382291944583158994)
XLA Ops:
  0.6 3.1 %shard_map.185 = f32[4352,128]{1,0:T(8,128)} custom-call(f32[8,2048]{1,0:T(8,128)} %image_hbm.1, f32[256,8,256]{2,1,0:T(8,128)} %bitcast.21, f32[8,256]{1,0:T(8,128)} %bitcast.22, s32[1,256]{1,0:T(1,128)} %bitcast.23, s32[1,256]{1,0:T(1,128)} %bitcast.24, f32[80,256]{1,0:T(8,128)} %constant.46.clone.turn_hbm), custom_call_target="tpu_custom_call" | custom-call | flops 200000000 | bytes 5000000 | tf_op jit(solution)/shard_map/pallas_call | solution.py:492
  3.7 71.7 %all_to_all.10 = f32[4352,1,128]{2,1,0:T(1,128)S(1)} all-to-all(f32[4352,1,128]{2,1,0:T(1,128)} %bitcast.20), channel_id=1, replica_groups={{0,64,128,192,194,130,66,2,4,68,132,196,198,134,70,6,22,86,150,214,212,..., dimensions={0} | all-to-all | bytes 4456448 | tf_op jit(solution)/shard_map/all_to_all | solution.py:455
  75.4 0.0 copy-start.3
  75.4 0.0 copy-start.4
  75.4 0.0 copy-start.10
  75.4 0.0 copy-start.13
  75.4 0.0 copy-start.14
  75.5 0.1 collective-permute-start
  75.6 0.8 shard_map.187
  76.3 0.0 copy-start
  76.3 0.5 collective-permute-done.other_ref
  76.9 0.0 copy-done.3
  76.9 0.0 copy-done.4
  76.9 0.0 copy-done.10
  76.9 0.0 copy-done.13
  76.9 0.0 copy-done.14
  76.9 0.0 copy-start.2
  76.9 2.6 %shard_map.188 = (f32[128,256]{1,0:T(8,128)}, f32[32,128]{1,0:T(8,128)}, f32[8,128]{1,0:T(8,128)S(1)}) custom-call(f32[128,256]{1,0:T(8,128)S(1)} %get-tuple-element.19.turned_ref, f32[256,128]{1,0:T(8,128)S(1)} %collective-permute-done.other_ref, bf16[2048,256]{1,0:T(8,128)(2,1)S(1)} %get-tuple-element.20.ah_ref, ...), custom_call_target="tpu_custom_call" | custom-call | flops 1000000000 | bytes 3000000 | tf_op jit(solution)/shard_map/pallas_call | solution.py:524
  79.5 0.0 copy-done
  79.5 0.0 copy-start.17
  79.5 0.6 copy-done.17
  80.1 0.2 collective-permute-start.1
  80.2 1.1 collective-permute-start.2
  81.3 2.4 %collective-permute-done.2.edge_ref = f32[32,128]{1,0:T(8,128)} collective-permute-done((f32[32,128]{1,0:T(8,128)}, f32[32,128]{1,0:T(8,128)}, u32[]{:S(2)}, u32[]{:S(2)}) %collective-permute-start.2) | collective-permute-done | bytes 16416 | tf_op jit(solution)/shard_map/ppermute | solution.py:462
  83.7 0.0 collective-permute-done.1.other_ref
  83.7 0.0 copy-done.2
  83.7 0.0 copy-start.1
  83.7 1.2 %copy-done.1 = bf16[256,2048]{1,0:T(8,128)(2,1)S(1)} copy-done((bf16[256,2048]{1,0:T(8,128)(2,1)S(1)}, bf16[256,2048]{1,0:T(8,128)(2,1)}, u32[]{:S(2)}) %copy-start.1) | copy-done | bytes 1048600
  85.0 0.0 copy-start.6
  85.0 0.8 copy-done.6
  85.8 0.0 copy-start.7
  85.8 2.6 %shard_map.189 = (f32[128,256]{1,0:T(8,128)S(1)}, f32[32,128]{1,0:T(8,128)S(1)}, f32[8,128]{1,0:T(8,128)S(1)}) custom-call(f32[128,256]{1,0:T(8,128)} %get-tuple-element.25.own_ref, f32[128,256]{1,0:T(8,128)} %collective-permute-done.1.other_ref, f32[32,128]{1,0:T(8,128)} %get-tuple-element.26.sent_ref, f32[32,128]{1,0:T(8,128)} %collective-permute-done.2.edge_ref, ...), custom_call_target="tpu_custom_call" | custom-call | flops 1000000000 | bytes 3000000 | tf_op jit(solution)/shard_map/pallas_call | solution.py:540
  88.4 1.7 %collective-permute-start.3 = (f32[128,256]{1,0:T(8,128)S(1)}, f32[128,256]{1,0:T(8,128)S(1)}, u32[]{:S(2)}, u32[]{:S(2)}) collective-permute-start(f32[128,256]{1,0:T(8,128)S(1)} %get-tuple-element.27.own_ref), channel_id=1, source_target_pairs={{0,8},{64,72},{128,136},{192,200},{194,202},{130,138},{66,74},{2,1... | collective-permute-start | bytes 393224 | tf_op jit(solution)/shard_map/ppermute | solution.py:463
  90.1 0.0 copy-start.5
  90.1 0.0 copy-start.11
  90.1 0.0 copy-start.15
  90.1 0.0 copy-start.16
  90.1 0.0 copy-start.18
  90.1 0.0 copy-start.8
  90.1 0.0 copy-start.9
  90.1 0.0 copy-start.12
  90.1 0.1 collective-permute-start.4
  90.2 3.4 %collective-permute-done.4.edge_ref = f32[32,128]{1,0:T(8,128)S(1)} collective-permute-done((f32[32,128]{1,0:T(8,128)S(1)}, f32[32,128]{1,0:T(8,128)S(1)}, u32[]{:S(2)}, u32[]{:S(2)}) %collective-permute-start.4) | collective-permute-done | bytes 16416 | tf_op jit(solution)/shard_map/ppermute | solution.py:462
  93.7 0.0 collective-permute-done.3.other_ref
  93.7 0.0 copy-done.7
  93.7 1.6 %shard_map.190 = (f32[128,256]{1,0:T(8,128)S(1)}, f32[32,128]{1,0:T(8,128)S(1)}, f32[8,128]{1,0:T(8,128)S(1)}) custom-call(f32[128,256]{1,0:T(8,128)S(1)} %get-tuple-element.27.own_ref, f32[128,256]{1,0:T(8,128)S(1)} %collective-permute-done.3.other_ref, f32[32,128]{1,0:T(8,128)S(1)} %get-tuple-element.28.sent_ref, ...), custom_call_target="tpu_custom_call" | custom-call | flops 1000000000 | bytes 3000000 | tf_op jit(solution)/shard_map/pallas_call | solution.py:540
  95.3 1.1 collective-permute-start.5
  96.3 0.0 collective-permute-start.6
  96.3 3.2 %collective-permute-done.6.edge_ref = f32[32,128]{1,0:T(8,128)S(1)} collective-permute-done((f32[32,128]{1,0:T(8,128)S(1)}, f32[32,128]{1,0:T(8,128)S(1)}, u32[]{:S(2)}, u32[]{:S(2)}) %collective-permute-start.6) | collective-permute-done | bytes 16416 | tf_op jit(solution)/shard_map/ppermute | solution.py:462
  99.5 0.0 collective-permute-done.5.other_ref
  99.5 0.0 copy-done.5
  99.5 0.0 copy-done.11
  99.5 0.0 copy-done.15
  99.5 0.0 copy-done.16
  99.5 0.0 copy-done.18
  99.5 1.2 %shard_map.191 = f32[256,128]{1,0:T(8,128)S(1)} custom-call(f32[128,256]{1,0:T(8,128)S(1)} %get-tuple-element.29.own_ref, f32[128,256]{1,0:T(8,128)S(1)} %collective-permute-done.5.other_ref, f32[32,128]{1,0:T(8,128)S(1)} %get-tuple-element.30.sent_ref, f32[32,128]{1,0:T(8,128)S(1)} %collective-permute-done.6.edge_ref, s32[1,1]{1,0:T(1,128)} %bitcast.8.alone_ref, ...), custom_call_target="tpu_custom_call" | custom-call | flops 300000000 | bytes 1500000 | tf_op jit(solution)/shard_map/pallas_call | solution.py:548
  100.8 19.0 %all_to_all.11 = f32[256,1,128]{2,1,0:T(1,128)S(1)} all-to-all(f32[256,1,128]{2,1,0:T(1,128)S(1)} %bitcast.18), channel_id=1, replica_groups={{0,64,128,192,194,130,66,2,4,68,132,196,198,134,70,6,22,86,150,214,212,..., dimensions={0} | all-to-all | bytes 262144 | tf_op jit(solution)/shard_map/all_to_all | solution.py:455
  119.8 0.0 copy-done.8
  119.8 0.0 copy-done.9
  119.8 0.0 copy-done.12
  119.8 1.0 shard_map.192
  (1 shorter events, 0.0 us)
Async XLA Ops:
  75.4 1.5 %copy-start.3 = (bf16[256,512]{1,0:T(8,128)(2,1)S(1)}, bf16[256,512]{1,0:T(8,128)(2,1)}, u32[]{:S(2)}) copy-start(bf16[256,512]{1,0:T(8,128)(2,1)} %constant.43.clone.th_ref) | copy-start | bytes 786436
  75.4 1.5 %copy-start.4 = (bf16[256,512]{1,0:T(8,128)(2,1)S(1)}, bf16[256,512]{1,0:T(8,128)(2,1)}, u32[]{:S(2)}) copy-start(bf16[256,512]{1,0:T(8,128)(2,1)} %constant.44.clone.tl_ref) | copy-start | bytes 786436
  75.4 1.5 %copy-start.10 = (f32[16,256]{1,0:T(8,128)S(1)}, f32[16,256]{1,0:T(8,128)}, u32[]{:S(2)}) copy-start(f32[16,256]{1,0:T(8,128)} %constant.45.clone.turn_ref) | copy-start | bytes 49156
  75.4 1.5 %copy-start.13 = (bf16[128,128]{1,0:T(8,128)(2,1)S(1)}, bf16[128,128]{1,0:T(8,128)(2,1)}, u32[]{:S(2)}) copy-start(bf16[128,128]{1,0:T(8,128)(2,1)} %constant.47.clone.eh_ref) | copy-start | bytes 98308
  75.4 1.5 %copy-start.14 = (bf16[128,128]{1,0:T(8,128)(2,1)S(1)}, bf16[128,128]{1,0:T(8,128)(2,1)}, u32[]{:S(2)}) copy-start(bf16[128,128]{1,0:T(8,128)(2,1)} %constant.48.clone.el_ref) | copy-start | bytes 98308
  75.5 1.4 %collective-permute-start = (f32[256,128]{1,0:T(8,128)S(1)}, f32[256,128]{1,0:T(8,128)S(1)}, u32[]{:S(2)}, u32[]{:S(2)}) collective-permute-start(f32[256,128]{1,0:T(8,128)S(1)} %shard_map.186.row_ref), channel_id=1, source_target_pairs={{0,8},{64,72},{128,136},{192,200},{194,202},{130,138},{66,74},{2,1... | collective-permute-start | bytes 393224 | tf_op jit(solution)/shard_map/ppermute | solution.py:502
  76.3 3.2 %copy-start = (bf16[256,2048]{1,0:T(8,128)(2,1)}, bf16[256,2048]{1,0:T(8,128)(2,1)S(1)}, u32[]{:S(2)}) copy-start(bf16[256,2048]{1,0:T(8,128)(2,1)S(1)} %get-tuple-element.23.bl_ref) | copy-start | bytes 3145732
  76.9 6.8 %copy-start.2 = (bf16[256,256]{1,0:T(8,128)(2,1)S(1)}, bf16[256,256]{1,0:T(8,128)(2,1)}, u32[]{:S(2)}) copy-start(bf16[256,256]{1,0:T(8,128)(2,1)} %constant.52.clone.fc_ref) | copy-start | bytes 393220
  79.5 0.6 copy-start.17
  80.1 3.6 %collective-permute-start.1 = (f32[128,256]{1,0:T(8,128)}, f32[128,256]{1,0:T(8,128)}, u32[]{:S(2)}, u32[]{:S(2)}) collective-permute-start(f32[128,256]{1,0:T(8,128)} %get-tuple-element.25.own_ref), channel_id=1, source_target_pairs={{0,8},{64,72},{128,136},{192,200},{194,202},{130,138},{66,74},{2,1... | collective-permute-start | bytes 393224 | tf_op jit(solution)/shard_map/ppermute | solution.py:463
  80.2 3.5 %collective-permute-start.2 = (f32[32,128]{1,0:T(8,128)}, f32[32,128]{1,0:T(8,128)}, u32[]{:S(2)}, u32[]{:S(2)}) collective-permute-start(f32[32,128]{1,0:T(8,128)} %get-tuple-element.26.sent_ref), channel_id=1, source_target_pairs={{0,57},{64,8},{128,72},{192,136},{194,200},{130,202},{66,138},{2,7... | collective-permute-start | bytes 49160 | tf_op jit(solution)/shard_map/ppermute | solution.py:462
  83.7 1.2 %copy-start.1 = (bf16[256,2048]{1,0:T(8,128)(2,1)S(1)}, bf16[256,2048]{1,0:T(8,128)(2,1)}, u32[]{:S(2)}) copy-start(bf16[256,2048]{1,0:T(8,128)(2,1)} %copy-done) | copy-start | bytes 3145732
  85.0 0.8 copy-start.6
  85.8 7.9 %copy-start.7 = (bf16[256,128]{1,0:T(8,128)(2,1)S(1)}, bf16[256,128]{1,0:T(8,128)(2,1)}, u32[]{:S(2)}) copy-start(bf16[256,128]{1,0:T(8,128)(2,1)} %constant.51.clone.ft_ref) | copy-start | bytes 196612
  88.4 5.3 %collective-permute-start.3 = (f32[128,256]{1,0:T(8,128)S(1)}, f32[128,256]{1,0:T(8,128)S(1)}, u32[]{:S(2)}, u32[]{:S(2)}) collective-permute-start(f32[128,256]{1,0:T(8,128)S(1)} %get-tuple-element.27.own_ref), channel_id=1, source_target_pairs={{0,8},{64,72},{128,136},{192,200},{194,202},{130,138},{66,74},{2,1... | collective-permute-start | bytes 393224 | tf_op jit(solution)/shard_map/ppermute | solution.py:463
  90.1 9.4 %copy-start.5 = (bf16[256,512]{1,0:T(8,128)(2,1)S(1)}, bf16[256,512]{1,0:T(8,128)(2,1)}, u32[]{:S(2)}) copy-start(bf16[256,512]{1,0:T(8,128)(2,1)} %constant.44.clone.tl_ref) | copy-start | bytes 786436
  90.1 9.4 %copy-start.11 = (f32[16,256]{1,0:T(8,128)S(1)}, f32[16,256]{1,0:T(8,128)}, u32[]{:S(2)}) copy-start(f32[16,256]{1,0:T(8,128)} %constant.45.clone.turn_ref) | copy-start | bytes 49156
  90.1 9.4 %copy-start.15 = (bf16[128,128]{1,0:T(8,128)(2,1)S(1)}, bf16[128,128]{1,0:T(8,128)(2,1)}, u32[]{:S(2)}) copy-start(bf16[128,128]{1,0:T(8,128)(2,1)} %constant.49.clone.eh_ref) | copy-start | bytes 98308
  90.1 9.5 %copy-start.16 = (bf16[128,128]{1,0:T(8,128)(2,1)S(1)}, bf16[128,128]{1,0:T(8,128)(2,1)}, u32[]{:S(2)}) copy-start(bf16[128,128]{1,0:T(8,128)(2,1)} %constant.50.clone.el_ref) | copy-start | bytes 98308
  90.1 9.5 %copy-start.18 = (f32[8,128]{1,0:T(8,128)S(1)}, f32[8,128]{1,0:T(8,128)}, u32[]{:S(2)}) copy-start(f32[8,128]{1,0:T(8,128)} %copy-done.17) | copy-start | bytes 12292
  90.1 29.7 %copy-start.8 = (bf16[256,512]{1,0:T(8,128)(2,1)S(1)}, bf16[256,512]{1,0:T(8,128)(2,1)}, u32[]{:S(2)}) copy-start(bf16[256,512]{1,0:T(8,128)(2,1)} %constant.41.clone.th_ref) | copy-start | bytes 786436
  90.1 29.7 %copy-start.9 = (bf16[256,512]{1,0:T(8,128)(2,1)S(1)}, bf16[256,512]{1,0:T(8,128)(2,1)}, u32[]{:S(2)}) copy-start(bf16[256,512]{1,0:T(8,128)(2,1)} %constant.42.clone.tl_ref) | copy-start | bytes 786436
  90.1 29.7 %copy-start.12 = (f32[256,128]{1,0:T(8,128)S(1)}, f32[256,128]{1,0:T(8,128)}, u32[]{:S(2)}) copy-start(f32[256,128]{1,0:T(8,128)} %constant.53.clone.share_ref) | copy-start | bytes 393220
  90.1 3.5 %collective-permute-start.4 = (f32[32,128]{1,0:T(8,128)S(1)}, f32[32,128]{1,0:T(8,128)S(1)}, u32[]{:S(2)}, u32[]{:S(2)}) collective-permute-start(f32[32,128]{1,0:T(8,128)S(1)} %get-tuple-element.28.sent_ref), channel_id=1, source_target_pairs={{0,57},{64,8},{128,72},{192,136},{194,200},{130,202},{66,138},{2,7... | collective-permute-start | bytes 49160 | tf_op jit(solution)/shard_map/ppermute | solution.py:462
  95.3 4.2 %collective-permute-start.5 = (f32[128,256]{1,0:T(8,128)S(1)}, f32[128,256]{1,0:T(8,128)S(1)}, u32[]{:S(2)}, u32[]{:S(2)}) collective-permute-start(f32[128,256]{1,0:T(8,128)S(1)} %get-tuple-element.29.own_ref), channel_id=1, source_target_pairs={{0,8},{64,72},{128,136},{192,200},{194,202},{130,138},{66,74},{2,1... | collective-permute-start | bytes 393224 | tf_op jit(solution)/shard_map/ppermute | solution.py:463
  96.3 3.2 %collective-permute-start.6 = (f32[32,128]{1,0:T(8,128)S(1)}, f32[32,128]{1,0:T(8,128)S(1)}, u32[]{:S(2)}, u32[]{:S(2)}) collective-permute-start(f32[32,128]{1,0:T(8,128)S(1)} %get-tuple-element.30.sent_ref), channel_id=1, source_target_pairs={{0,57},{64,8},{128,72},{192,136},{194,200},{130,202},{66,138},{2,7... | collective-permute-start | bytes 49160 | tf_op jit(solution)/shard_map/ppermute | solution.py:462

commit v6 on v4

--- a/solution.py
+++ b/solution.py
@@ -402,7 +402,7 @@
     out_ref[...] = out
 
 
-def last_kernel(got_ref, share_ref, th_ref, tl_ref, turn_ref, image_ref, found_ref):
+def last_kernel(got_ref, share_ref, th_ref, tl_ref, turn_ref, image_hbm, found_ref, image_ref, sems):
     got = got_ref[...]
     totals = jnp.sum(got, axis=0, keepdims=True)
     norms = [jnp.sqrt(totals[:, NORM_LANE + i : NORM_LANE + i + 1]) for i in range(4)]
@@ -421,6 +421,7 @@
         cos, sin = turn_ref[c : c + 1, :] * factor, turn_ref[8 + c : 9 + c, :] * factor
         re.append(r * cos - i * sin)
         im.append(i * cos + r * sin)
+    sent = []
     for j in range(8):
         total = re[0]
         for c in range(1, 5):
@@ -428,6 +429,14 @@
             sin = math.sin(2.0 * math.pi * (c * j % 8) / 8)
             total = total + re[c] * cos - im[c] * sin
         image_ref[:, j * 256 : (j + 1) * 256] = total
+        if j % 4 == 3:
+            part = pl.ds((j - 3) * 256, 1024)
+            sent.append(
+                pltpu.make_async_copy(image_ref.at[:, part], image_hbm.at[:, part], sems.at[j // 4])
+            )
+            sent[-1].start()
+    for copy in sent:
+        copy.wait()
 
 
 def call(kernel, outs, in_specs, flops, moved, scratch=(), limit=24 * 2**20, out_specs=None):
@@ -541,6 +550,8 @@
         [VMEM] * 5,
         200_000_000,
         1_500_000,
+        scratch=[pltpu.VMEM((ROWS, N), F32), pltpu.SemaphoreType.DMA((2,))],
+        out_specs=(HBM, VMEM),
     )
     image, found = last(got, t["share"], *t["plain"], t["turn"])
     return image, found.reshape(3)

time: 117 us -> 118 us (level)
  no operation moved by 1% of the time
where the time goes in v6:
time: 118 us
  blocking collectives  90.6 us (77%)
  Pallas kernels  12.4 us (11%)
  waiting for transfers between devices  9.21 us (8%)
  starting transfers between devices  4.52 us (4%)
    all_to_all x2, blocking collectives, exchange(): lax.all_to_all(message.reshape(rows, 1, LANES), AXES, 0, 0, tiled=True, a...  90.6 us
    ppermute x3, waiting for transfers between devices, mirror_exchange(): got = lax.ppermute(edge, AXES, MIRROR_EDGE)  8.37 us
    pallas_call x2, Pallas kernels, per_device(): follow(*blocks, a_high, a_low, mask, t['flip_tile'], t['flip_cell'])  3.73 us
    ppermute x3, starting transfers between devices, mirror_exchange(): other = lax.ppermute(grid, AXES, MIRROR)  3.32 us
    pallas_call x1, Pallas kernels, per_device(): pack(image0, interp.reshape(SLOTS, VCAP, CELLS), vis_weight.reshape(SLOTS...  3.08 us
    pallas_call x1, Pallas kernels, per_device(): first(turned, other, a_high, a_low, mask, *t['placed'], t['turn'], *t['ei...  2.38 us
  transfers between devices with their start and end apart: 7, of which 4 were waited for; matrix products, arithmetic and copies ran while one was open for 0% of the time, Pallas kernels for 0%

profile of v6, /device:TPU:1, one launch (start us, length us, event | category | flops | bytes accessed | tf_op | source)
XLA Modules:
  0.0 117.6 jit_solution(2332869529329589905)
XLA Ops:
  0.6 3.1 %shard_map.185 = f32[4352,128]{1,0:T(8,128)} custom-call(f32[8,2048]{1,0:T(8,128)} %image_hbm.1, f32[256,8,256]{2,1,0:T(8,128)} %bitcast.21, f32[8,256]{1,0:T(8,128)} %bitcast.22, s32[1,256]{1,0:T(1,128)} %bitcast.23, s32[1,256]{1,0:T(1,128)} %bitcast.24, f32[80,256]{1,0:T(8,128)} %constant.46.clone.turn_hbm), custom_call_target="tpu_custom_call" | custom-call | flops 200000000 | bytes 5000000 | tf_op jit(solution)/shard_map/pallas_call | solution.py:493
  3.7 71.7 %all_to_all.10 = f32[4352,1,128]{2,1,0:T(1,128)S(1)} all-to-all(f32[4352,1,128]{2,1,0:T(1,128)} %bitcast.20), channel_id=1, replica_groups={{0,64,128,192,194,130,66,2,4,68,132,196,198,134,70,6,22,86,150,214,212,..., dimensions={0} | all-to-all | bytes 4456448 | tf_op jit(solution)/shard_map/all_to_all | solution.py:456
  75.4 0.0 copy-start.2
  75.4 0.0 copy-start.3
  75.4 0.0 copy-start.6
  75.4 0.0 copy-start.10
  75.4 0.0 copy-start.11
  75.4 0.1 collective-permute-start
  75.5 0.5 shard_map.187
  76.0 0.0 copy-start.5
  76.0 0.0 copy-start.7
  76.0 0.8 collective-permute-done.other_ref
  76.9 0.0 copy-done.2
  76.9 0.0 copy-done.3
  76.9 0.0 copy-done.6
  76.9 0.0 copy-done.10
  76.9 0.0 copy-done.11
  76.9 2.4 %shard_map.188 = (f32[128,256]{1,0:T(8,128)S(1)}, f32[32,128]{1,0:T(8,128)S(1)}, f32[8,128]{1,0:T(8,128)S(1)}) custom-call(f32[128,256]{1,0:T(8,128)S(1)} %get-tuple-element.17.turned_ref, f32[256,128]{1,0:T(8,128)S(1)} %collective-permute-done.other_ref, bf16[2048,256]{1,0:T(8,128)(2,1)S(1)} %get-tuple-element.18.ah_ref, ...), custom_call_target="tpu_custom_call" | custom-call | flops 1000000000 | bytes 3000000 | tf_op jit(solution)/shard_map/pallas_call | solution.py:518
  79.3 0.2 collective-permute-start.1
  79.5 1.1 collective-permute-start.2
  80.6 2.1 %collective-permute-done.2.edge_ref = f32[32,128]{1,0:T(8,128)S(1)} collective-permute-done((f32[32,128]{1,0:T(8,128)S(1)}, f32[32,128]{1,0:T(8,128)S(1)}, u32[]{:S(2)}, u32[]{:S(2)}) %collective-permute-start.2) | collective-permute-done | bytes 16416 | tf_op jit(solution)/shard_map/ppermute | solution.py:463
  82.7 0.0 collective-permute-done.1.other_ref
  82.7 0.0 copy-done.5
  82.7 0.0 copy-done.7
  82.7 1.9 %shard_map.189 = (f32[128,256]{1,0:T(8,128)S(1)}, f32[32,128]{1,0:T(8,128)S(1)}, f32[8,128]{1,0:T(8,128)S(1)}) custom-call(f32[128,256]{1,0:T(8,128)S(1)} %get-tuple-element.21.own_ref, f32[128,256]{1,0:T(8,128)S(1)} %collective-permute-done.1.other_ref, f32[32,128]{1,0:T(8,128)S(1)} %get-tuple-element.22.sent_ref, ...), custom_call_target="tpu_custom_call" | custom-call | flops 1000000000 | bytes 3000000 | tf_op jit(solution)/shard_map/pallas_call | solution.py:534
  84.6 0.0 copy-start.8
  84.6 0.0 copy-start.9
  84.6 1.7 %collective-permute-start.3 = (f32[128,256]{1,0:T(8,128)S(1)}, f32[128,256]{1,0:T(8,128)S(1)}, u32[]{:S(2)}, u32[]{:S(2)}) collective-permute-start(f32[128,256]{1,0:T(8,128)S(1)} %get-tuple-element.23.own_ref), channel_id=1, source_target_pairs={{0,8},{64,72},{128,136},{192,200},{194,202},{130,138},{66,74},{2,1... | collective-permute-start | bytes 393224 | tf_op jit(solution)/shard_map/ppermute | solution.py:464
  86.2 0.0 copy-start
  86.2 0.0 copy-start.1
  86.2 0.0 copy-start.4
  86.3 0.0 collective-permute-start.4
  86.3 3.2 %collective-permute-done.4.edge_ref = f32[32,128]{1,0:T(8,128)S(1)} collective-permute-done((f32[32,128]{1,0:T(8,128)S(1)}, f32[32,128]{1,0:T(8,128)S(1)}, u32[]{:S(2)}, u32[]{:S(2)}) %collective-permute-start.4) | collective-permute-done | bytes 16416 | tf_op jit(solution)/shard_map/ppermute | solution.py:463
  89.4 0.0 collective-permute-done.3.other_ref
  89.4 1.9 %shard_map.190 = (f32[128,256]{1,0:T(8,128)S(1)}, f32[32,128]{1,0:T(8,128)S(1)}, f32[8,128]{1,0:T(8,128)S(1)}) custom-call(f32[128,256]{1,0:T(8,128)S(1)} %get-tuple-element.23.own_ref, f32[128,256]{1,0:T(8,128)S(1)} %collective-permute-done.3.other_ref, f32[32,128]{1,0:T(8,128)S(1)} %get-tuple-element.24.sent_ref, ...), custom_call_target="tpu_custom_call" | custom-call | flops 1000000000 | bytes 3000000 | tf_op jit(solution)/shard_map/pallas_call | solution.py:534
  91.3 1.4 %collective-permute-start.5 = (f32[128,256]{1,0:T(8,128)S(1)}, f32[128,256]{1,0:T(8,128)S(1)}, u32[]{:S(2)}, u32[]{:S(2)}) collective-permute-start(f32[128,256]{1,0:T(8,128)S(1)} %get-tuple-element.25.own_ref), channel_id=1, source_target_pairs={{0,8},{64,72},{128,136},{192,200},{194,202},{130,138},{66,74},{2,1... | collective-permute-start | bytes 393224 | tf_op jit(solution)/shard_map/ppermute | solution.py:464
  92.7 0.0 collective-permute-start.6
  92.7 3.2 %collective-permute-done.6.edge_ref = f32[32,128]{1,0:T(8,128)S(1)} collective-permute-done((f32[32,128]{1,0:T(8,128)S(1)}, f32[32,128]{1,0:T(8,128)S(1)}, u32[]{:S(2)}, u32[]{:S(2)}) %collective-permute-start.6) | collective-permute-done | bytes 16416 | tf_op jit(solution)/shard_map/ppermute | solution.py:463
  95.9 0.0 collective-permute-done.5.other_ref
  95.9 0.0 copy-done.8
  95.9 0.0 copy-done.9
  95.9 1.2 %shard_map.191 = f32[256,128]{1,0:T(8,128)S(1)} custom-call(f32[128,256]{1,0:T(8,128)S(1)} %get-tuple-element.25.own_ref, f32[128,256]{1,0:T(8,128)S(1)} %collective-permute-done.5.other_ref, f32[32,128]{1,0:T(8,128)S(1)} %get-tuple-element.26.sent_ref, f32[32,128]{1,0:T(8,128)S(1)} %collective-permute-done.6.edge_ref, s32[1,1]{1,0:T(1,128)} %bitcast.8.alone_ref, ...), custom_call_target="tpu_custom_call" | custom-call | flops 300000000 | bytes 1500000 | tf_op jit(solution)/shard_map/pallas_call | solution.py:542
  97.1 19.0 %all_to_all.11 = f32[256,1,128]{2,1,0:T(1,128)S(1)} all-to-all(f32[256,1,128]{2,1,0:T(1,128)S(1)} %bitcast.18), channel_id=1, replica_groups={{0,64,128,192,194,130,66,2,4,68,132,196,198,134,70,6,22,86,150,214,212,..., dimensions={0} | all-to-all | bytes 262144 | tf_op jit(solution)/shard_map/all_to_all | solution.py:456
  116.1 0.0 copy-done
  116.1 0.0 copy-done.1
  116.1 0.0 copy-done.4
  116.1 1.5 %shard_map.192 = (f32[8,2048]{1,0:T(8,128)}, f32[1,3]{1,0:T(1,128)}) custom-call(f32[256,128]{1,0:T(8,128)S(1)} %bitcast.19, f32[256,128]{1,0:T(8,128)S(1)} %copy-done.4, bf16[256,512]{1,0:T(8,128)(2,1)S(1)} %copy-done, bf16[256,512]{1,0:T(8,128)(2,1)S(1)} %copy-done.1, f32[16,256]{1,0:T(8,128)S(1)} %copy-done.6), custom_call_target="tpu_custom_call" | custom-call | flops 200000000 | bytes 1500000 | tf_op jit(solution)/shard_map/pallas_call | solution.py:556
  (1 shorter events, 0.0 us)
Async XLA Ops:
  75.4 1.5 %copy-start.2 = (bf16[256,512]{1,0:T(8,128)(2,1)S(1)}, bf16[256,512]{1,0:T(8,128)(2,1)}, u32[]{:S(2)}) copy-start(bf16[256,512]{1,0:T(8,128)(2,1)} %constant.43.clone.th_ref) | copy-start | bytes 786436
  75.4 1.5 %copy-start.3 = (bf16[256,512]{1,0:T(8,128)(2,1)S(1)}, bf16[256,512]{1,0:T(8,128)(2,1)}, u32[]{:S(2)}) copy-start(bf16[256,512]{1,0:T(8,128)(2,1)} %constant.44.clone.tl_ref) | copy-start | bytes 786436
  75.4 1.5 %copy-start.6 = (f32[16,256]{1,0:T(8,128)S(1)}, f32[16,256]{1,0:T(8,128)}, u32[]{:S(2)}) copy-start(f32[16,256]{1,0:T(8,128)} %constant.45.clone.turn_ref) | copy-start | bytes 49156
  75.4 1.5 %copy-start.10 = (bf16[128,128]{1,0:T(8,128)(2,1)S(1)}, bf16[128,128]{1,0:T(8,128)(2,1)}, u32[]{:S(2)}) copy-start(bf16[128,128]{1,0:T(8,128)(2,1)} %constant.47.clone.eh_ref) | copy-start | bytes 98308
  75.4 1.5 %copy-start.11 = (bf16[128,128]{1,0:T(8,128)(2,1)S(1)}, bf16[128,128]{1,0:T(8,128)(2,1)}, u32[]{:S(2)}) copy-start(bf16[128,128]{1,0:T(8,128)(2,1)} %constant.48.clone.el_ref) | copy-start | bytes 98308
  75.4 1.4 %collective-permute-start = (f32[256,128]{1,0:T(8,128)S(1)}, f32[256,128]{1,0:T(8,128)S(1)}, u32[]{:S(2)}, u32[]{:S(2)}) collective-permute-start(f32[256,128]{1,0:T(8,128)S(1)} %shard_map.186.row_ref), channel_id=1, source_target_pairs={{0,8},{64,72},{128,136},{192,200},{194,202},{130,138},{66,74},{2,1... | collective-permute-start | bytes 393224 | tf_op jit(solution)/shard_map/ppermute | solution.py:503
  76.0 6.7 %copy-start.5 = (bf16[256,256]{1,0:T(8,128)(2,1)S(1)}, bf16[256,256]{1,0:T(8,128)(2,1)}, u32[]{:S(2)}) copy-start(bf16[256,256]{1,0:T(8,128)(2,1)} %constant.52.clone.fc_ref) | copy-start | bytes 393220
  76.0 6.7 %copy-start.7 = (bf16[256,128]{1,0:T(8,128)(2,1)S(1)}, bf16[256,128]{1,0:T(8,128)(2,1)}, u32[]{:S(2)}) copy-start(bf16[256,128]{1,0:T(8,128)(2,1)} %constant.51.clone.ft_ref) | copy-start | bytes 196612
  79.3 3.4 %collective-permute-start.1 = (f32[128,256]{1,0:T(8,128)S(1)}, f32[128,256]{1,0:T(8,128)S(1)}, u32[]{:S(2)}, u32[]{:S(2)}) collective-permute-start(f32[128,256]{1,0:T(8,128)S(1)} %get-tuple-element.21.own_ref), channel_id=1, source_target_pairs={{0,8},{64,72},{128,136},{192,200},{194,202},{130,138},{66,74},{2,1... | collective-permute-start | bytes 393224 | tf_op jit(solution)/shard_map/ppermute | solution.py:464
  79.5 3.2 %collective-permute-start.2 = (f32[32,128]{1,0:T(8,128)S(1)}, f32[32,128]{1,0:T(8,128)S(1)}, u32[]{:S(2)}, u32[]{:S(2)}) collective-permute-start(f32[32,128]{1,0:T(8,128)S(1)} %get-tuple-element.22.sent_ref), channel_id=1, source_target_pairs={{0,57},{64,8},{128,72},{192,136},{194,200},{130,202},{66,138},{2,7... | collective-permute-start | bytes 49160 | tf_op jit(solution)/shard_map/ppermute | solution.py:463
  84.6 11.3 %copy-start.8 = (bf16[128,128]{1,0:T(8,128)(2,1)S(1)}, bf16[128,128]{1,0:T(8,128)(2,1)}, u32[]{:S(2)}) copy-start(bf16[128,128]{1,0:T(8,128)(2,1)} %constant.49.clone.eh_ref) | copy-start | bytes 98308
  84.6 11.3 %copy-start.9 = (bf16[128,128]{1,0:T(8,128)(2,1)S(1)}, bf16[128,128]{1,0:T(8,128)(2,1)}, u32[]{:S(2)}) copy-start(bf16[128,128]{1,0:T(8,128)(2,1)} %constant.50.clone.el_ref) | copy-start | bytes 98308
  84.6 4.8 %collective-permute-start.3 = (f32[128,256]{1,0:T(8,128)S(1)}, f32[128,256]{1,0:T(8,128)S(1)}, u32[]{:S(2)}, u32[]{:S(2)}) collective-permute-start(f32[128,256]{1,0:T(8,128)S(1)} %get-tuple-element.23.own_ref), channel_id=1, source_target_pairs={{0,8},{64,72},{128,136},{192,200},{194,202},{130,138},{66,74},{2,1... | collective-permute-start | bytes 393224 | tf_op jit(solution)/shard_map/ppermute | solution.py:464
  86.2 29.9 %copy-start = (bf16[256,512]{1,0:T(8,128)(2,1)S(1)}, bf16[256,512]{1,0:T(8,128)(2,1)}, u32[]{:S(2)}) copy-start(bf16[256,512]{1,0:T(8,128)(2,1)} %constant.41.clone.th_ref) | copy-start | bytes 786436
  86.2 29.9 %copy-start.1 = (bf16[256,512]{1,0:T(8,128)(2,1)S(1)}, bf16[256,512]{1,0:T(8,128)(2,1)}, u32[]{:S(2)}) copy-start(bf16[256,512]{1,0:T(8,128)(2,1)} %constant.42.clone.tl_ref) | copy-start | bytes 786436
  86.2 29.9 %copy-start.4 = (f32[256,128]{1,0:T(8,128)S(1)}, f32[256,128]{1,0:T(8,128)}, u32[]{:S(2)}) copy-start(f32[256,128]{1,0:T(8,128)} %constant.53.clone.share_ref) | copy-start | bytes 393220
  86.3 3.2 %collective-permute-start.4 = (f32[32,128]{1,0:T(8,128)S(1)}, f32[32,128]{1,0:T(8,128)S(1)}, u32[]{:S(2)}, u32[]{:S(2)}) collective-permute-start(f32[32,128]{1,0:T(8,128)S(1)} %get-tuple-element.24.sent_ref), channel_id=1, source_target_pairs={{0,57},{64,8},{128,72},{192,136},{194,200},{130,202},{66,138},{2,7... | collective-permute-start | bytes 49160 | tf_op jit(solution)/shard_map/ppermute | solution.py:463
  91.3 4.6 %collective-permute-start.5 = (f32[128,256]{1,0:T(8,128)S(1)}, f32[128,256]{1,0:T(8,128)S(1)}, u32[]{:S(2)}, u32[]{:S(2)}) collective-permute-start(f32[128,256]{1,0:T(8,128)S(1)} %get-tuple-element.25.own_ref), channel_id=1, source_target_pairs={{0,8},{64,72},{128,136},{192,200},{194,202},{130,138},{66,74},{2,1... | collective-permute-start | bytes 393224 | tf_op jit(solution)/shard_map/ppermute | solution.py:464
  92.7 3.2 %collective-permute-start.6 = (f32[32,128]{1,0:T(8,128)S(1)}, f32[32,128]{1,0:T(8,128)S(1)}, u32[]{:S(2)}, u32[]{:S(2)}) collective-permute-start(f32[32,128]{1,0:T(8,128)S(1)} %get-tuple-element.26.sent_ref), channel_id=1, source_target_pairs={{0,57},{64,8},{128,72},{192,136},{194,200},{130,202},{66,138},{2,7... | collective-permute-start | bytes 49160 | tf_op jit(solution)/shard_map/ppermute | solution.py:463
